TPU v7x, 32 devices: a whole 2x2x4 slice. The times are simulated.
32 devices in a mesh: group: 8 (over z, y), peer: 4 (over x, core).
Axes of the slice: x: 2, y: 2, z: 4, core: 2. Of those that a mesh axis runs over, the one named last changes fastest.
Arguments:
- features: float32 [128, 64, 384], P('group', 'peer'), may hold values from -6 to 6
- image_of_row: int32 [8], replicated, may hold values from 0 to 3, never falling along the last dimension, each value on 1 to 4 neighbouring positions
- llm_peer: int32 [32, 1], P(('group', 'peer')), may hold values from 0 to 3, as said below
- token_grads: float32 [64, 64, 384], P(('group', 'peer')), may hold values from -6 to 6
- dw_weight: float32 [49, 384], replicated, may hold values from -0.875 to 0.875
- dw_bias: float32 [384], replicated, may hold values from -3 to 3
- ln_gain: float32 [384], replicated, may hold values from 0.1 to 1.9
- ln_bias: float32 [384], replicated, may hold values from -3 to 3
- w_in: bfloat16 [384, 1536], replicated, may hold values from -0.3125 to 0.3125
- b_in: float32 [1536], replicated, may hold values from -3 to 3
- w_out: bfloat16 [1536, 384], replicated, may hold values from -0.15625 to 0.15625
- b_out: float32 [384], replicated, may hold values from -3 to 3
- layer_scale: float32 [384], replicated, may hold values from 0.3 to 1
- comp_weight: bfloat16 [9, 384, 384], replicated, may hold values from -0.109375 to 0.109375
- comp_bias: float32 [384], replicated, may hold values from -3 to 3
Outputs:
- llm_tokens: float32 [64, 64, 384], P(('group', 'peer'))
- feature_grads: float32 [128, 64, 384], P('group', 'peer')
Inputs may be any that keep to these rules, and one draw needn't show every extreme that they name: `llm_peer`: the 1 tiles of one device go to 1 different peers of its group; each peer receives at most 2 tiles of its tile row, and in tile row 0 some peer receives exactly 2. `image_of_row`: Non-decreasing along tile rows; each image spans 1 to 4 consecutive tile rows.
All inputs are finite; a program needn't handle non-finite values.
Results may differ from a plain program's by a relative error of at most 0.005.
Values sent between devices are 32-bit elements; how exact they have to be, the bound alone decides.
A program may use at most 64 MiB of HBM per device.

v0:
```python
import functools
import math

import jax
import jax.numpy as jnp
from jax import lax
from jax.experimental import pallas as pl
from jax.experimental.pallas import tpu as pltpu
from jax.sharding import PartitionSpec as P

MESH = pl.DeviceIdType.MESH
LANES = 128
PAD = 8
BLOCK = 256
ROWS = ((-1, -1), (-1, 0), (-1, 1), (0, -1), (0, 1), (1, -1), (1, 0), (1, 1))


def nt_dot(a, b):
    return lax.dot_general(a, b, (((1,), (1,)), ((), ())), preferred_element_type=jnp.float32)


def depthwise(src, weight, chunk, taps, side, flip):
    half = side // 2
    reach = taps // 2
    outs = []
    for parity in range(2):
        total = None
        for b in range(taps):
            rows = src[chunk, :, pl.ds(PAD - reach + parity + b, half, stride=2), :]
            for a in range(taps):
                k = (taps - 1 - a) * taps + taps - 1 - b if flip else a * taps + b
                term = rows[a : a + side] * weight[chunk, k : k + 1, :]
                total = term if total is None else total + term
        outs.append(total)
    return outs


def kernel(
    groups,
    peers,
    taps,
    image_hbm,
    owner_hbm,
    x_hbm,
    tg_hbm,
    dww_hbm,
    dwb_hbm,
    gain_hbm,
    lnb_hbm,
    win_hbm,
    bin_hbm,
    wout_hbm,
    bout_hbm,
    scale_hbm,
    cw_hbm,
    cb_hbm,
    gpad,
    dww,
    gq,
    tokout,
    xpad,
    dwb,
    gain,
    lnb,
    bout,
    scale,
    cb,
    bin_,
    win,
    wout,
    cw,
    tg,
    sp,
    rstd,
    nb,
    dg,
    hb,
    dpb,
    table,
    sendg,
    recvg,
    sendf,
    recvf,
    tok,
    recvt,
    recvr,
    grid_g,
    grid_p,
    col_g,
    col_p,
    halo_g,
    halo_p,
    image_ref,
    owner_ref,
    in_sems,
    tab_send,
    tab_recv,
    near_send,
    near_recv,
    g_send,
    g_recv,
    t_send,
    t_recv,
    r_send,
    r_recv,
    hg_send,
    hg_recv,
    hp_send,
    hp_recv,
):
    g = lax.axis_index("group")
    me = lax.axis_index("peer")
    side = x_hbm.shape[0]
    channels = x_hbm.shape[2]
    half = side // 2
    cells = half * half
    chunks = channels // LANES
    reach = taps // 2
    hid = win.shape[1]
    slots = tg.shape[0]
    small = (dwb, gain, lnb, bout, scale, cb)

    def vector(ref, lane=slice(None)):
        return ref[lane].reshape(1, -1)

    halo_g[...] = jnp.zeros_like(halo_g)
    halo_p[...] = jnp.zeros_like(halo_p)
    barrier = pltpu.get_barrier_semaphore()

    def there(dr, dp):
        conds = []
        if dr < 0:
            conds.append(g > 0)
        if dr > 0:
            conds.append(g < groups - 1)
        if dp < 0:
            conds.append(me > 0)
        if dp > 0:
            conds.append(me < peers - 1)
        cond = conds[0]
        for other in conds[1:]:
            cond = jnp.logical_and(cond, other)
        return cond

    for k in range(1, peers):
        pl.semaphore_signal(
            barrier, inc=1, device_id={"group": g, "peer": lax.rem(me + k, peers)}, device_id_type=MESH
        )
    for dr, dp in ROWS:
        if dr != 0:

            @pl.when(there(dr, dp))
            def _():
                pl.semaphore_signal(
                    barrier, inc=1, device_id={"group": g + dr, "peer": me + dp}, device_id_type=MESH
                )

    copies = {}

    def fetch(name, src, dst):
        copy = pltpu.make_async_copy(src, dst, in_sems.at[len(copies)])
        copy.start()
        copies[name] = copy

    fetch("owner", owner_hbm, owner_ref)
    for c in range(chunks):
        lane = slice(c * LANES, (c + 1) * LANES)
        fetch(("w", c), dww_hbm.at[:, lane], dww.at[c])
        fetch(("x", c), x_hbm.at[:, :, lane], xpad.at[c, reach : reach + side, PAD : PAD + side, :])
    for i, src in enumerate((dwb_hbm, gain_hbm, lnb_hbm, bout_hbm, scale_hbm, cb_hbm)):
        fetch(("s", i), src, small[i])
    fetch("tg", tg_hbm, tg)
    fetch("image", image_hbm, image_ref)
    fetch("bin", bin_hbm, bin_)
    fetch("win", win_hbm, win)
    fetch("wout", wout_hbm, wout)
    fetch("cw", cw_hbm, cw)

    def clear(buf):
        width = buf.shape[2]
        for c in range(chunks):
            buf[c, :reach] = jnp.zeros((reach, width, LANES), jnp.float32)
            buf[c, reach + side :] = jnp.zeros((reach, width, LANES), jnp.float32)
            buf[c, reach : reach + side, :PAD] = jnp.zeros((side, PAD, LANES), jnp.float32)
            buf[c, reach : reach + side, PAD + side :] = jnp.zeros((side, PAD, LANES), jnp.float32)

    clear(xpad)
    clear(gpad)
    copies["owner"].wait()
    own = owner_ref[0, 0]
    table[me] = jnp.full((8, LANES), own, jnp.int32)

    def forward_conv(c):
        outs = depthwise(xpad, dww, c, taps, side, False)
        bias = vector(small[0], slice(c * LANES, (c + 1) * LANES))
        for parity in range(2):
            part = (outs[parity] + bias).reshape(half, 2, half, LANES)
            for row in range(2):
                sp[c, row * 2 + parity] = part[:, row].reshape(cells, LANES)

    across = 1 + (me > 0).astype(jnp.int32) + (me < peers - 1).astype(jnp.int32)
    along = (g > 0).astype(jnp.int32) + (g < groups - 1).astype(jnp.int32)
    pl.semaphore_wait(barrier, peers - 1 + across * along)

    table_moves = []
    for k in range(1, peers):
        table_moves.append(
            pltpu.make_async_remote_copy(
                src_ref=table.at[me],
                dst_ref=table.at[me],
                send_sem=tab_send.at[k - 1],
                recv_sem=tab_recv.at[k - 1],
                device_id={"group": g, "peer": lax.rem(me + k, peers)},
                device_id_type=MESH,
            )
        )
        table_moves[-1].start()
    copies[("s", 0)].wait()
    for c in range(chunks):
        copies[("w", c)].wait()
        copies[("x", c)].wait()
        forward_conv(c)
    for move in table_moves:
        move.wait()
    copies["tg"].wait()

    def place_of(who):
        mine = table[who] == me
        before = jnp.zeros((8, LANES), jnp.int32)
        for p in range(peers):
            earlier = (p < who).astype(jnp.int32)
            before = before + jnp.where(table[p] == me, earlier, 0)
        return mine, before

    def wide(mask):
        return jnp.concatenate([mask.astype(jnp.float32)] * chunks, axis=1)

    def block_for(who):
        mine, before = place_of(who)
        total = None
        for s in range(slots):
            part = tg[s] * wide(jnp.logical_and(mine, before == s))
            total = part if total is None else total + part
        return total

    pairs = peers // 2
    core = lax.rem(me, 2)
    partner = me + 1 - 2 * core

    def seat(k, which):
        return lax.rem(lax.div(me, 2) + k, pairs) * 2 + which

    def to(src, dst, send, recv, where):
        return pltpu.make_async_remote_copy(
            src_ref=src,
            dst_ref=dst,
            send_sem=send,
            recv_sem=recv,
            device_id={"group": g, "peer": where},
            device_id_type=MESH,
        )

    for k in range(pairs):
        sendg[k] = block_for(seat(k, 1 - core))
    near_move = to(sendg, recvg, near_send, near_recv, partner)
    near_move.start()
    grid_g[1 : half + 1, PAD : PAD + half, :] = block_for(me)
    far_moves = [
        to(sendf.at[k - 1], recvf.at[k - 1], g_send.at[k - 1], g_recv.at[k - 1], seat(k, core))
        for k in range(1, pairs)
    ]

    def pass_on():
        near_move.wait()
        for k in range(1, pairs):
            sendf[k - 1] = block_for(seat(k, core)) + recvg[k]
            far_moves[k - 1].start()

    for i in range(1, 6):
        copies[("s", i)].wait()
    for q in range(4):
        parts = [sp[c, q] for c in range(chunks)]
        mean = jnp.sum(functools.reduce(jnp.add, parts), axis=1, keepdims=True) / channels
        parts = [part - mean for part in parts]
        square = functools.reduce(jnp.add, [part * part for part in parts])
        inv = lax.rsqrt(jnp.sum(square, axis=1, keepdims=True) / channels + 1e-06)
        rstd[q] = jnp.broadcast_to(inv, (cells, LANES))
        for c in range(chunks):
            lane = slice(c * LANES, (c + 1) * LANES)
            hat = parts[c] * inv
            sp[c, q] = hat
            nb[q * cells : (q + 1) * cells, lane] = (
                hat * vector(small[1], lane) + vector(small[2], lane)
            ).astype(jnp.bfloat16)

    def halo_moves(grid, col, halo, send, recv):
        moves = []
        for i, (dr, dp) in enumerate(ROWS):
            if dr == 0:
                src = col.at[0 if dp < 0 else 1]
            else:
                src = grid.at[1 if dr < 0 else half, PAD : PAD + half, :]
            back = len(ROWS) - 1 - i
            moves.append(
                pltpu.make_async_remote_copy(
                    src_ref=src,
                    dst_ref=halo.at[back],
                    send_sem=send.at[i],
                    recv_sem=recv.at[back],
                    device_id={"group": g + dr, "peer": me + dp},
                    device_id_type=MESH,
                )
            )
        return moves

    def halo_start(grid, col, moves):
        col[0] = grid[1 : half + 1, PAD, :]
        col[1] = grid[1 : half + 1, PAD + half - 1, :]
        for (dr, dp), move in zip(ROWS, moves):

            @pl.when(there(dr, dp))
            def _():
                move.start()

    def halo_finish(grid, halo, moves, send, recv):
        for i, (dr, dp) in enumerate(ROWS):

            @pl.when(there(dr, dp))
            def _():
                moves[i].wait_send()
                pltpu.make_async_remote_copy(
                    src_ref=halo.at[i],
                    dst_ref=halo.at[i],
                    send_sem=send.at[i],
                    recv_sem=recv.at[i],
                    device_id={"group": g + dr, "peer": me + dp},
                    device_id_type=MESH,
                ).wait_recv()

        image = image_ref[g]
        keep = {
            -1: (image_ref[jnp.maximum(g - 1, 0)] == image).astype(jnp.float32) * (g > 0).astype(jnp.float32),
            0: 1.0,
            1: (image_ref[jnp.minimum(g + 1, groups - 1)] == image).astype(jnp.float32)
            * (g < groups - 1).astype(jnp.float32),
        }
        edge = {-1: (me > 0).astype(jnp.float32), 0: 1.0, 1: (me < peers - 1).astype(jnp.float32)}
        for i, (dr, dp) in enumerate(ROWS):
            row = {-1: 0, 1: half + 1}.get(dr)
            factor = keep[dr] * edge[dp]
            if dr == 0:
                grid[1 : half + 1, PAD - 1 if dp < 0 else PAD + half, :] = halo[i] * factor
            elif dp == 0:
                grid[row, PAD : PAD + half, :] = halo[i] * factor
            elif dp < 0:
                grid[row, PAD - 1 : PAD, :] = halo[i, half - 1 : half, :] * factor
            else:
                grid[row, PAD + half : PAD + half + 1, :] = halo[i, 0:1, :] * factor

    def window(grid, a, b):
        part = grid[a : a + half, PAD - 1 + b : PAD - 1 + b + half, :]
        return part.reshape(cells, channels).astype(jnp.bfloat16)

    g_moves = halo_moves(grid_g, col_g, halo_g, hg_send, hg_recv)
    p_moves = halo_moves(grid_p, col_p, halo_p, hp_send, hp_recv)

    def gather_grads():
        total = grid_g[1 : half + 1, PAD : PAD + half, :] + recvg[0]
        for k in range(1, pairs):
            far_moves[k - 1].wait()
            total = total + recvf[k - 1]
        grid_g[1 : half + 1, PAD : PAD + half, :] = total
        halo_start(grid_g, col_g, g_moves)

    copies["bin"].wait()
    copies["image"].wait()
    copies["win"].wait()
    for n in range(hid // BLOCK):
        lane = slice(n * BLOCK, (n + 1) * BLOCK)
        pre_all = jnp.dot(nb[...], win[:, lane], preferred_element_type=jnp.float32)
        bias = vector(bin_, lane)
        pooled = None
        for q in range(4):
            pre = pre_all[q * cells : (q + 1) * cells] + bias
            cdf = 0.5 + 0.5 * lax.erf(pre * math.sqrt(0.5))
            pdf = jnp.exp(pre * pre * -0.5) * (1.0 / math.sqrt(2.0 * math.pi))
            dg[q * cells : (q + 1) * cells, lane] = cdf + pre * pdf
            value = pre * cdf
            pooled = value if pooled is None else pooled + value
        hb[:, lane] = (pooled * 0.25).astype(jnp.bfloat16)
        if n == hid // BLOCK - 2:
            pass_on()
    copies["wout"].wait()
    branch = jnp.dot(hb[...], wout[...], preferred_element_type=jnp.float32)
    for c in range(chunks):
        lane = slice(c * LANES, (c + 1) * LANES)
        total = None
        for row in range(2):
            for parity in range(2):
                part = xpad[c, reach : reach + side, pl.ds(PAD + parity, half, stride=2), :]
                part = part.reshape(half, 2, half, LANES)[:, row]
                total = part if total is None else total + part
        mixed = vector(small[4], lane) * (branch[:, lane] + vector(small[3], lane))
        grid_p[1 : half + 1, PAD : PAD + half, lane] = total * 0.25 + mixed.reshape(half, half, LANES)
    halo_start(grid_p, col_p, p_moves)

    copies["cw"].wait()
    halo_finish(grid_p, halo_p, p_moves, hp_send, hp_recv)
    comp = None
    for a in range(3):
        for b in range(3):
            part = jnp.dot(window(grid_p, a, b), cw[a * 3 + b], preferred_element_type=jnp.float32)
            comp = part if comp is None else comp + part
    tok[...] = (comp + vector(cb)).reshape(half, half, channels)
    tok_moves = [to(tok, recvt.at[0], t_send.at[0], t_recv.at[0], partner)]
    for k in range(1, pairs):
        tok_moves.append(to(tok, recvt.at[k], t_send.at[k], t_recv.at[k], seat(k, core)))
    for move in reversed(tok_moves):
        move.start()
    gather_grads()

    halo_finish(grid_g, halo_g, g_moves, hg_send, hg_recv)
    grads = None
    for a in range(3):
        for b in range(3):
            part = nt_dot(window(grid_g, a, b), cw[(2 - a) * 3 + 2 - b])
            grads = part if grads is None else grads + part
    grads = grads * 0.25
    for c in range(chunks):
        lane = slice(c * LANES, (c + 1) * LANES)
        gq[c] = grads[:, lane].reshape(half, half, LANES)
    scaled = (grads * vector(scale)).astype(jnp.bfloat16)

    relays = []

    def relay():
        for k in range(1, pairs):
            tok_moves[k].wait()
            relays.append(to(recvt.at[k], recvr.at[k - 1], r_send.at[k - 1], r_recv.at[k - 1], partner))
            relays[-1].start()

    for n in range(hid // BLOCK):
        lane = slice(n * BLOCK, (n + 1) * BLOCK)
        dh = nt_dot(scaled, wout[lane, :])
        for q in range(4):
            rows = slice(q * cells, (q + 1) * cells)
            dpb[rows, lane] = (dh * dg[rows, lane]).astype(jnp.bfloat16)
    relay()
    for q in range(4):
        dn = nt_dot(dpb[q * cells : (q + 1) * cells, :], win[...]) * vector(gain)
        parts = [dn[:, c * LANES : (c + 1) * LANES] for c in range(chunks)]
        first = jnp.sum(functools.reduce(jnp.add, parts), axis=1, keepdims=True) / channels
        cross = functools.reduce(jnp.add, [parts[c] * sp[c, q] for c in range(chunks)])
        second = jnp.sum(cross, axis=1, keepdims=True) / channels
        for c in range(chunks):
            back = rstd[q] * (parts[c] - first - sp[c, q] * second)
            back = back.reshape(half, half, LANES)
            for i in range(half):
                gpad[c, reach + 2 * i + q // 2, pl.ds(PAD + q % 2, half, stride=2), :] = back[i]

    tok_moves[0].wait()
    for move in relays:
        move.wait()
    arrived = [(me, tok), (partner, recvt.at[0])]
    for k in range(1, pairs):
        arrived.append((seat(pairs - k, core), recvt.at[k]))
        arrived.append((seat(pairs - k, 1 - core), recvr.at[k - 1]))
    outs = [None] * slots
    for who, block in arrived:
        mine, before = place_of(who)
        for s in range(slots):
            part = block[...] * wide(jnp.logical_and(mine, before == s))
            outs[s] = part if outs[s] is None else outs[s] + part
    for s in range(slots):
        tokout[s] = outs[s]


def tail(taps, gpad, dww, gq, tokout, tok_hbm, dx_hbm, obuf, sems):
    chunks = gpad.shape[0]
    side = dx_hbm.shape[0]
    half = side // 2
    copies = [pltpu.make_async_copy(tokout, tok_hbm, sems.at[chunks])]
    copies[0].start()
    for c in range(chunks):
        outs = depthwise(gpad, dww, c, taps, side, True)
        direct = jnp.broadcast_to(gq[c][:, None], (half, 2, half, LANES)).reshape(side, half, LANES)
        for parity in range(2):
            value = outs[parity] + direct
            for i in range(side):
                obuf[c, i, pl.ds(parity, half, stride=2), :] = value[i]
        copy = pltpu.make_async_copy(
            obuf.at[c], dx_hbm.at[:, :, c * LANES : (c + 1) * LANES], sems.at[c]
        )
        copy.start()
        copies.append(copy)
    for copy in copies:
        copy.wait()


def solution(mesh):
    groups, peers = mesh.shape["group"], mesh.shape["peer"]

    def on_device(
        features, image_of_row, llm_peer, token_grads, dw_weight, dw_bias, ln_gain, ln_bias,
        w_in, b_in, w_out, b_out, layer_scale, comp_weight, comp_bias,
    ):
        side, width, channels = features.shape
        slots = token_grads.shape[0]
        hid = w_in.shape[1]
        taps = math.isqrt(dw_weight.shape[0])
        half = side // 2
        cells = half * half
        chunks = channels // LANES
        assert width == side and llm_peer.shape == (1, 1)
        f32, bf16 = jnp.float32, jnp.bfloat16
        padded = (chunks, side + 2 * (taps // 2), side + 2 * PAD, LANES)
        grid = (half + 2, half + 2 * PAD, channels)
        block = (half, half, channels)
        dma = pltpu.SemaphoreType.DMA
        hbm = pl.BlockSpec(memory_space=pltpu.HBM)
        pairs = peers // 2
        assert peers == 2 * pairs and pairs > 1
        vmem = pl.BlockSpec(memory_space=pltpu.VMEM)
        held = (
            pltpu.VMEM(padded, f32),
            pltpu.VMEM((chunks, taps * taps, LANES), f32),
            pltpu.VMEM((chunks, half, half, LANES), f32),
            pltpu.VMEM((slots,) + block, f32),
        )
        state = pl.pallas_call(
            functools.partial(kernel, groups, peers, taps),
            out_shape=held,
            in_specs=[hbm] * 15,
            out_specs=(vmem,) * 4,
            scratch_shapes=[
                pltpu.VMEM(padded, f32),
                *[pltpu.VMEM((channels,), f32)] * 6,
                pltpu.VMEM((hid,), f32),
                pltpu.VMEM(w_in.shape, bf16),
                pltpu.VMEM(w_out.shape, bf16),
                pltpu.VMEM(comp_weight.shape, bf16),
                pltpu.VMEM((slots,) + block, f32),
                pltpu.VMEM((chunks, 4, cells, LANES), f32),
                pltpu.VMEM((4, cells, LANES), f32),
                pltpu.VMEM((4 * cells, channels), bf16),
                pltpu.VMEM((4 * cells, hid), f32),
                pltpu.VMEM((cells, hid), bf16),
                pltpu.VMEM((4 * cells, hid), bf16),
                pltpu.VMEM((peers, 8, LANES), jnp.int32),
                pltpu.VMEM((pairs,) + block, f32),
                pltpu.VMEM((pairs,) + block, f32),
                pltpu.VMEM((pairs - 1,) + block, f32),
                pltpu.VMEM((pairs - 1,) + block, f32),
                pltpu.VMEM(block, f32),
                pltpu.VMEM((pairs,) + block, f32),
                pltpu.VMEM((pairs - 1,) + block, f32),
                pltpu.VMEM(grid, f32),
                pltpu.VMEM(grid, f32),
                pltpu.VMEM((2, half, channels), f32),
                pltpu.VMEM((2, half, channels), f32),
                pltpu.VMEM((8, half, channels), f32),
                pltpu.VMEM((8, half, channels), f32),
                pltpu.SMEM(image_of_row.shape, jnp.int32),
                pltpu.SMEM((1, 1), jnp.int32),
                dma((2 * chunks + 13,)),
                dma((peers - 1,)),
                dma((peers - 1,)),
                dma,
                dma,
                dma((pairs - 1,)),
                dma((pairs - 1,)),
                dma((pairs,)),
                dma((pairs,)),
                dma((pairs - 1,)),
                dma((pairs - 1,)),
                dma((8,)),
                dma((8,)),
                dma((8,)),
                dma((8,)),
            ],
            compiler_params=pltpu.CompilerParams(collective_id=0, has_side_effects=True),
        )(
            image_of_row,
            llm_peer,
            features,
            token_grads.reshape((slots,) + block),
            dw_weight,
            dw_bias,
            ln_gain,
            ln_bias,
            w_in,
            b_in,
            w_out,
            b_out,
            layer_scale,
            comp_weight,
            comp_bias,
        )
        tokens, grads = pl.pallas_call(
            functools.partial(tail, taps),
            out_shape=(
                jax.ShapeDtypeStruct((slots,) + block, f32),
                jax.ShapeDtypeStruct(features.shape, f32),
            ),
            in_specs=[vmem] * 4,
            out_specs=(hbm, hbm),
            scratch_shapes=[pltpu.VMEM((chunks, side, side, LANES), f32), dma((chunks + 1,))],
            compiler_params=pltpu.CompilerParams(vmem_limit_bytes=16 << 20),
        )(*state)
        return tokens.reshape(slots, cells, channels), grads

    placed = [P()] * 15
    placed[0] = P("group", "peer", None)
    placed[2] = P(("group", "peer"), None)
    placed[3] = P(("group", "peer"), None, None)
    return jax.shard_map(
        on_device,
        mesh=mesh,
        in_specs=tuple(placed),
        out_specs=(P(("group", "peer"), None, None), P("group", "peer", None)),
        check_vma=False,
    )
```

profile of v0, /device:TPU:1, one launch (start us, length us, event | category | flops | bytes accessed | tf_op | source)
XLA Modules:
  0.0 24.5 jit_solution(16038661313562220491)
XLA Ops:
  1.3 20.9 %shard_map.158 = (f32[3,22,32,128]{3,2,1,0:T(8,128)S(1)}, f32[3,49,128]{2,1,0:T(8,128)S(1)}, f32[3,8,8,128]{3,2,1,0:T(8,128)S(1)}, f32[2,8,8,384]{3,2,1,0:T(8,128)S(1)}) custom-call(s32[8]{0:T(128)} %image_hbm.1, s32[1,1]{1,0:T(1,128)S(6)} %copy.17.owner_hbm, f32[16,16,384]{2,1,0:T(8,128)} %x_hbm.1, f32[2,8,8,384]{3,2,1,0:T(8,128)} %bitcast.2, ...), custom_call_target="tpu_custom_call" | custom-call | tf_op jit(solution)/shard_map/pallas_call | solution.py:530
  22.1 2.3 %shard_map.159 = (f32[2,8,8,384]{3,2,1,0:T(8,128)}, f32[16,16,384]{2,1,0:T(8,128)}) custom-call(f32[3,22,32,128]{3,2,1,0:T(8,128)S(1)} %get-tuple-element.8.gpad, f32[3,49,128]{2,1,0:T(8,128)S(1)} %get-tuple-element.9.dww, f32[3,8,8,128]{3,2,1,0:T(8,128)S(1)} %get-tuple-element.10.gq, f32[2,8,8,384]{3,2,1,0:T(8,128)S(1)} %get-tuple-element.11.tokout), custom_call_target="tpu_custom_call" | custom-call | tf_op jit(solution)/shard_map/pallas_call | solution.py:599
where the time goes:
time: 24.6 us; the launch traced here: 24.5 us
  Pallas kernels  23.2 us (94%)
  between operations  1.29 us (5%)
    pallas_call x1, Pallas kernels, on_device(): pl.pallas_call(functools.partial(kernel, groups, peers, taps), out_shape=...  20.9 us
    pallas_call x1, Pallas kernels, on_device(): pl.pallas_call(functools.partial(tail, taps), out_shape=(jax.ShapeDtypeSt...  2.32 us

commit v1 on v0

v1 whole, which is shorter than its diff:
```python
import functools
import math
import types

import jax
import jax.numpy as jnp
from jax import lax
from jax.experimental import pallas as pl
from jax.experimental.pallas import tpu as pltpu
from jax.sharding import PartitionSpec as P

MESH = pl.DeviceIdType.MESH
LANES = 128
PAD = 8
BLOCK = 256
WIDE = 16


def nt_dot(a, b):
    return lax.dot_general(a, b, (((1,), (1,)), ((), ())), preferred_element_type=jnp.float32)


def depthwise(src, weight, chunk, taps, side, flip):
    half = side // 2
    reach = taps // 2
    outs = []
    for parity in range(2):
        total = None
        for b in range(taps):
            rows = src[chunk, :, pl.ds(PAD - reach + parity + b, half, stride=2), :]
            for a in range(taps):
                k = (taps - 1 - a) * taps + taps - 1 - b if flip else a * taps + b
                term = rows[a : a + side] * weight[chunk, k : k + 1, :]
                total = term if total is None else total + term
        outs.append(total)
    return outs


def kernel(groups, peers, taps, names, *refs):
    r = types.SimpleNamespace(**dict(zip(names, refs)))
    g = lax.axis_index("group")
    me = lax.axis_index("peer")
    side = r.x_hbm.shape[0]
    channels = r.x_hbm.shape[2]
    half = side // 2
    cells = half * half
    chunks = channels // LANES
    reach = taps // 2
    hid = r.win.shape[1]
    slots = r.tg.shape[0]
    pairs = peers // 2
    core = lax.rem(me, 2)
    partner = me + 1 - 2 * core
    small = (r.dwb, r.gain, r.lnb, r.bout, r.scale, r.cb)
    inner = slice(PAD, PAD + half)

    def vector(ref, lane=slice(None)):
        return ref[lane].reshape(1, -1)

    def seat(k, which):
        return lax.rem(lax.div(me, 2) + k, pairs) * 2 + which

    beyond = {-1: g > 0, 1: g < groups - 1}

    for buf in (r.grow, r.gcorn_in, r.arow, r.acorn):
        buf[...] = jnp.zeros_like(buf)
    barrier = pltpu.get_barrier_semaphore()

    def greet(row, who):
        pl.semaphore_signal(barrier, inc=1, device_id={"group": row, "peer": who}, device_id_type=MESH)

    for k in range(1, peers):
        greet(g, lax.rem(me + k, peers))
    for dr in (-1, 1):

        @pl.when(beyond[dr])
        def _():
            for k in range(pairs):
                greet(g + dr, seat(k, core))

    copies = {}

    def fetch(name, src, dst):
        copy = pltpu.make_async_copy(src, dst, r.in_sems.at[len(copies)])
        copy.start()
        copies[name] = copy

    fetch("owner", r.owner_hbm, r.owner_ref)
    fetch("tg", r.tg_hbm, r.tg)
    for c in range(chunks):
        lane = slice(c * LANES, (c + 1) * LANES)
        fetch(("w", c), r.dww_hbm.at[:, lane], r.dww.at[c])
        fetch(("x", c), r.x_hbm.at[:, :, lane], r.xpad.at[c, reach : reach + side, PAD : PAD + side, :])
    for i, src in enumerate((r.dwb_hbm, r.gain_hbm, r.lnb_hbm, r.bout_hbm, r.scale_hbm, r.cb_hbm)):
        fetch(("s", i), src, small[i])
    fetch("image", r.image_hbm, r.image_ref)
    fetch("bin", r.bin_hbm, r.bin_)
    fetch("win", r.win_hbm, r.win)
    fetch("wout", r.wout_hbm, r.wout)
    fetch("cw", r.cw_hbm, r.cw)

    def clear(buf):
        width = buf.shape[2]
        for c in range(chunks):
            buf[c, :reach] = jnp.zeros((reach, width, LANES), jnp.float32)
            buf[c, reach + side :] = jnp.zeros((reach, width, LANES), jnp.float32)
            buf[c, reach : reach + side, :PAD] = jnp.zeros((side, PAD, LANES), jnp.float32)
            buf[c, reach : reach + side, PAD + side :] = jnp.zeros((side, PAD, LANES), jnp.float32)

    clear(r.xpad)
    clear(r.gpad)
    r.grid_p[...] = jnp.zeros_like(r.grid_p)

    def move(src, dst, sems, index, where, row=None):
        send, recv = sems
        return pltpu.make_async_remote_copy(
            src_ref=src,
            dst_ref=dst,
            send_sem=send.at[index],
            recv_sem=recv.at[index],
            device_id={"group": g if row is None else row, "peer": where},
            device_id_type=MESH,
        )

    copies["owner"].wait()
    r.table[me] = jnp.full((8, LANES), r.owner_ref[0, 0], jnp.int32)
    along = (g > 0).astype(jnp.int32) + (g < groups - 1).astype(jnp.int32)
    pl.semaphore_wait(barrier, peers - 1 + pairs * along)

    tab_sems = (r.tab_send, r.tab_recv)
    table_moves = [
        move(r.table.at[me], r.table.at[me], tab_sems, k - 1, lax.rem(me + k, peers)) for k in range(1, peers)
    ]
    for m in table_moves:
        m.start()
    copies["tg"].wait()
    near_move = move(r.tg, r.ntg, (r.near_send, r.near_recv), 0, partner)
    near_move.start()

    def forward_conv(c):
        outs = depthwise(r.xpad, r.dww, c, taps, side, False)
        bias = vector(small[0], slice(c * LANES, (c + 1) * LANES))
        for parity in range(2):
            part = (outs[parity] + bias).reshape(half, 2, half, LANES)
            for row in range(2):
                r.sp[c, row * 2 + parity] = part[:, row].reshape(cells, LANES)

    copies[("s", 0)].wait()
    for c in range(chunks):
        copies[("w", c)].wait()
        copies[("x", c)].wait()
        forward_conv(c)
    for m in table_moves:
        m.wait()
    near_move.wait()

    def masks_of(who, device):
        inside = jnp.logical_and(who >= 0, who < peers)
        at = jnp.clip(who, 0, peers - 1)
        mine = jnp.logical_and(r.table[at] == device, inside)
        before = jnp.zeros((8, LANES), jnp.int32)
        for p in range(peers):
            earlier = (p < at).astype(jnp.int32)
            before = before + jnp.where(r.table[p] == device, earlier, 0)
        return [jnp.logical_and(mine, before == s).astype(jnp.float32) for s in range(slots)]

    def wide(mask):
        return jnp.concatenate([mask] * chunks, axis=1)

    def held(who):
        pairs_of = []
        for ref, device in ((r.tg, me), (r.ntg, partner)):
            for s, mask in enumerate(masks_of(who, device)):
                pairs_of.append((ref, s, wide(mask)))
        return pairs_of

    def total_of(terms):
        return functools.reduce(jnp.add, terms)

    for k in range(pairs):
        home = seat(k, core)
        r.gmain[k] = total_of([ref[s] * mask for ref, s, mask in held(home)])
        left = total_of([ref[s, :, half - 1, :] * mask for ref, s, mask in held(home - 1)])
        right = total_of([ref[s, :, 0, :] * mask for ref, s, mask in held(home + 1)])
        r.gcols[k, 0] = left
        r.gcols[k, 1] = right
        for d, at in ((0, 0), (1, half - 1)):
            r.gcorn[k, d, 0:1, :] = left[at : at + 1]
            r.gcorn[k, d, 1:2, :] = right[at : at + 1]

    row_sems = (r.row_send, r.row_recv)
    cor_sems = (r.cor_send, r.cor_recv)

    def row_moves(src_row, src_corner, dst_row, dst_corner, sems_r, sems_c):
        moves = {}
        for d, dr in ((0, -1), (1, 1)):
            for k in range(pairs):
                moves[d, k] = (
                    move(src_row(d, k), dst_row(d, k), sems_r, d * pairs + k, seat(k, core), g + dr),
                    move(src_corner(d, k), dst_corner(d, k), sems_c, d * pairs + k, seat(k, core), g + dr),
                )
        return moves

    def start_rows(moves):
        for d, dr in ((0, -1), (1, 1)):

            @pl.when(beyond[dr])
            def _():
                for k in reversed(range(pairs)):
                    for m in moves[d, k]:
                        m.start()

    def sent_rows(moves):
        for d, dr in ((0, -1), (1, 1)):

            @pl.when(beyond[dr])
            def _():
                for k in range(pairs):
                    for m in moves[d, k]:
                        m.wait_send()

    def received_rows(moves):
        for d, dr in ((0, -1), (1, 1)):

            @pl.when(beyond[-dr])
            def _():
                for k in range(pairs):
                    for m in moves[d, k]:
                        m.wait_recv()

    g_rows = row_moves(
        lambda d, k: r.gmain.at[k, 0 if d == 0 else half - 1],
        lambda d, k: r.gcorn.at[k, d],
        lambda d, k: r.grow.at[d, k],
        lambda d, k: r.gcorn_in.at[d, k],
        row_sems,
        cor_sems,
    )
    start_rows(g_rows)
    far_sems = (r.far_send, r.far_recv)
    g_far = []
    for k in range(1, pairs):
        g_far.append(move(r.gcols.at[k], r.rcols.at[k - 1], far_sems, 2 * k - 2, seat(k, core)))
        g_far.append(move(r.gmain.at[k], r.rmain.at[k - 1], far_sems, 2 * k - 1, seat(k, core)))
    for m in g_far:
        m.start()

    for i in range(1, 6):
        copies[("s", i)].wait()
    for q in range(4):
        parts = [r.sp[c, q] for c in range(chunks)]
        mean = jnp.sum(functools.reduce(jnp.add, parts), axis=1, keepdims=True) / channels
        parts = [part - mean for part in parts]
        square = functools.reduce(jnp.add, [part * part for part in parts])
        inv = lax.rsqrt(jnp.sum(square, axis=1, keepdims=True) / channels + 1e-06)
        r.rstd[q] = jnp.broadcast_to(inv, (cells, LANES))
        for c in range(chunks):
            lane = slice(c * LANES, (c + 1) * LANES)
            hat = parts[c] * inv
            r.sp[c, q] = hat
            r.nb[q * cells : (q + 1) * cells, lane] = (
                hat * vector(small[1], lane) + vector(small[2], lane)
            ).astype(jnp.bfloat16)

    copies["bin"].wait()
    copies["image"].wait()
    copies["win"].wait()
    for n in range(hid // BLOCK):
        lane = slice(n * BLOCK, (n + 1) * BLOCK)
        pre_all = jnp.dot(r.nb[...], r.win[:, lane], preferred_element_type=jnp.float32)
        bias = vector(r.bin_, lane)
        pooled = None
        for q in range(4):
            pre = pre_all[q * cells : (q + 1) * cells] + bias
            cdf = 0.5 + 0.5 * lax.erf(pre * math.sqrt(0.5))
            pdf = jnp.exp(pre * pre * -0.5) * (1.0 / math.sqrt(2.0 * math.pi))
            r.dg[q * cells : (q + 1) * cells, lane] = cdf + pre * pdf
            value = pre * cdf
            pooled = value if pooled is None else pooled + value
        r.hb[:, lane] = (pooled * 0.25).astype(jnp.bfloat16)
    copies["wout"].wait()
    branch = jnp.dot(r.hb[...], r.wout[...], preferred_element_type=jnp.float32)
    for c in range(chunks):
        lane = slice(c * LANES, (c + 1) * LANES)
        total = None
        for row in range(2):
            for parity in range(2):
                part = r.xpad[c, reach : reach + side, pl.ds(PAD + parity, half, stride=2), :]
                part = part.reshape(half, 2, half, LANES)[:, row]
                total = part if total is None else total + part
        mixed = vector(small[4], lane) * (branch[:, lane] + vector(small[3], lane))
        r.grid_p[2 : half + 2, inner, lane] = total * 0.25 + mixed.reshape(half, half, LANES)

    copies["cw"].wait()
    rim = half + 2
    comp = None
    for a in range(3):
        for b in range(3):
            part = r.grid_p[a : a + rim, PAD - 2 + b : PAD - 2 + b + WIDE, :]
            part = part.reshape(rim * WIDE, channels).astype(jnp.bfloat16)
            part = jnp.dot(part, r.cw[a * 3 + b], preferred_element_type=jnp.float32)
            comp = part if comp is None else comp + part
    comp = comp.reshape(rim, WIDE, channels)
    r.amain[me] = comp[1 : half + 1, 1 : half + 1]
    for d, at in ((0, 0), (1, half + 1)):
        r.acols[me, d] = comp[1 : half + 1, at]
        r.erow[d] = comp[at, 1 : half + 1]
        r.ecorn[d, 0:1, :] = comp[at, 0:1]
        r.ecorn[d, 1:2, :] = comp[at, half + 1 : half + 2]

    trow_sems = (r.trow_send, r.trow_recv)
    tcor_sems = (r.tcor_send, r.tcor_recv)
    t_rows = row_moves(
        lambda d, k: r.erow.at[d],
        lambda d, k: r.ecorn.at[d],
        lambda d, k: r.arow.at[d, me],
        lambda d, k: r.acorn.at[d, me],
        trow_sems,
        tcor_sems,
    )
    start_rows(t_rows)
    tok_sems = (r.tok_send, r.tok_recv)
    t_far = []
    for k in range(1, pairs):
        t_far.append(move(r.acols.at[me], r.acols.at[me], tok_sems, 2 * k, seat(k, core)))
        t_far.append(move(r.amain.at[me], r.amain.at[me], tok_sems, 2 * k + 1, seat(k, core)))
    t_near = [
        move(r.acols.at[me], r.acols.at[me], tok_sems, 0, partner),
        move(r.amain.at[me], r.amain.at[me], tok_sems, 1, partner),
    ]
    for m in t_far + t_near:
        m.start()

    image = r.image_ref[g]
    keep = {}
    for d, near in ((1, jnp.maximum(g - 1, 0)), (0, jnp.minimum(g + 1, groups - 1))):
        there = (g > 0) if d == 1 else (g < groups - 1)
        keep[d] = (r.image_ref[near] == image).astype(jnp.float32) * there.astype(jnp.float32)

    received_rows(g_rows)
    for m in g_far:
        m.wait_recv()
    def far(own, other):
        return total_of([own] + [other(k) for k in range(pairs - 1)])
    r.grid_g[1 : half + 1, inner, :] = far(r.gmain[0], lambda k: r.rmain[k])
    r.grid_g[1 : half + 1, PAD - 1, :] = far(r.gcols[0, 0], lambda k: r.rcols[k, 0])
    r.grid_g[1 : half + 1, PAD + half, :] = far(r.gcols[0, 1], lambda k: r.rcols[k, 1])
    for d, row in ((1, 0), (0, half + 1)):
        r.grid_g[row, inner, :] = total_of([r.grow[d, k] for k in range(pairs)]) * keep[d]
        corner = total_of([r.gcorn_in[d, k] for k in range(pairs)]) * keep[d]
        r.grid_g[row, PAD - 1 : PAD, :] = corner[0:1]
        r.grid_g[row, PAD + half : PAD + half + 1, :] = corner[1:2]

    grads = None
    for a in range(3):
        for b in range(3):
            part = r.grid_g[a : a + half, PAD - 1 + b : PAD - 1 + b + half, :]
            part = part.reshape(cells, channels).astype(jnp.bfloat16)
            part = nt_dot(part, r.cw[(2 - a) * 3 + 2 - b])
            grads = part if grads is None else grads + part
    grads = grads * 0.25
    for c in range(chunks):
        lane = slice(c * LANES, (c + 1) * LANES)
        r.gq[c] = grads[:, lane].reshape(half, half, LANES)
    scaled = (grads * vector(r.scale)).astype(jnp.bfloat16)

    for n in range(hid // BLOCK):
        lane = slice(n * BLOCK, (n + 1) * BLOCK)
        dh = nt_dot(scaled, r.wout[lane, :])
        for q in range(4):
            rows = slice(q * cells, (q + 1) * cells)
            r.dpb[rows, lane] = (dh * r.dg[rows, lane]).astype(jnp.bfloat16)
    dn_all = nt_dot(r.dpb[...], r.win[...])
    for q in range(4):
        dn = dn_all[q * cells : (q + 1) * cells] * vector(r.gain)
        parts = [dn[:, c * LANES : (c + 1) * LANES] for c in range(chunks)]
        first = jnp.sum(functools.reduce(jnp.add, parts), axis=1, keepdims=True) / channels
        cross = functools.reduce(jnp.add, [parts[c] * r.sp[c, q] for c in range(chunks)])
        second = jnp.sum(cross, axis=1, keepdims=True) / channels
        for c in range(chunks):
            back = r.rstd[q] * (parts[c] - first - r.sp[c, q] * second)
            back = back.reshape(half, half, LANES)
            for i in range(half):
                r.gpad[c, reach + 2 * i + q // 2, pl.ds(PAD + q % 2, half, stride=2), :] = back[i]

    def backward_conv(c):
        outs = depthwise(r.gpad, r.dww, c, taps, side, True)
        direct = jnp.broadcast_to(r.gq[c][:, None], (half, 2, half, LANES)).reshape(side, half, LANES)
        for parity in range(2):
            value = outs[parity] + direct
            for i in range(side):
                r.obuf[c, i, pl.ds(parity, half, stride=2), :] = value[i]

    for c in range(chunks - 1):
        backward_conv(c)

    received_rows(t_rows)
    for m in t_far:
        m.wait_recv()
    pass_sems = (r.pass_send, r.pass_recv)
    passed = []
    for k in range(1, pairs):
        who = seat(pairs - k, core)
        passed.append(move(r.acols.at[who], r.acols.at[who], pass_sems, 2 * k - 2, partner))
        passed.append(move(r.amain.at[who], r.amain.at[who], pass_sems, 2 * k - 1, partner))
    for m in passed:
        m.start()
    prow_sems = (r.prow_send, r.prow_recv)
    pcor_sems = (r.pcor_send, r.pcor_recv)
    passed_rows = {}
    for d, dr in ((0, -1), (1, 1)):
        for k in range(pairs):
            who = seat(k, core)
            passed_rows[d, k] = (
                move(r.arow.at[d, who], r.arow.at[d, who], prow_sems, d * pairs + k, partner),
                move(r.acorn.at[d, who], r.acorn.at[d, who], pcor_sems, d * pairs + k, partner),
            )
        @pl.when(beyond[-dr])
        def _():
            for k in range(pairs):
                for m in passed_rows[d, k]:
                    m.start()

    backward_conv(chunks - 1)

    for m in t_near + passed:
        m.wait()
    for m in t_far + g_far:
        m.wait_send()
    sent_rows(g_rows)
    sent_rows(t_rows)
    for d, dr in ((0, -1), (1, 1)):

        @pl.when(beyond[-dr])
        def _():
            for k in range(pairs):
                for m in passed_rows[d, k]:
                    m.wait()

    chosen = [[wide(mask) for mask in masks_of(p, me)] for p in range(peers)]
    bias = vector(r.cb)
    for s in range(slots):
        total = None
        west = jnp.zeros((half, channels), jnp.float32)
        east = jnp.zeros((half, channels), jnp.float32)
        line = {d: jnp.zeros((half, channels), jnp.float32) for d in range(2)}
        tips = {d: [jnp.zeros((1, channels), jnp.float32) for _ in range(2)] for d in range(2)}
        for p in range(peers):
            mask = chosen[p][s]
            part = (r.amain[p] + bias) * mask
            total = part if total is None else total + part
            if p > 0:
                west = west + r.acols[p - 1, 1] * mask
            if p < peers - 1:
                east = east + r.acols[p + 1, 0] * mask
            for d in range(2):
                line[d] = line[d] + r.arow[d, p] * mask
                if p > 0:
                    tips[d][0] = tips[d][0] + r.acorn[d, p - 1, 1:2, :] * mask[:1]
                if p < peers - 1:
                    tips[d][1] = tips[d][1] + r.acorn[d, p + 1, 0:1, :] * mask[:1]
        r.tokout[s] = total
        r.tokout[s, :, 0, :] += west
        r.tokout[s, :, half - 1, :] += east
        for d, row in ((1, 0), (0, half - 1)):
            r.tokout[s, row] += line[d] * keep[d]
            r.tokout[s, row, 0:1, :] += tips[d][0] * keep[d]
            r.tokout[s, row, half - 1 : half, :] += tips[d][1] * keep[d]


def tail(obuf, tokout, tok_hbm, dx_hbm, sems):
    chunks = obuf.shape[0]
    copies = [pltpu.make_async_copy(tokout, tok_hbm, sems.at[chunks])]
    for c in range(chunks):
        copies.append(
            pltpu.make_async_copy(obuf.at[c], dx_hbm.at[:, :, c * LANES : (c + 1) * LANES], sems.at[c])
        )
    for copy in copies:
        copy.start()
    for copy in copies:
        copy.wait()


def solution(mesh):
    groups, peers = mesh.shape["group"], mesh.shape["peer"]

    def on_device(
        features, image_of_row, llm_peer, token_grads, dw_weight, dw_bias, ln_gain, ln_bias,
        w_in, b_in, w_out, b_out, layer_scale, comp_weight, comp_bias,
    ):
        side, width, channels = features.shape
        slots = token_grads.shape[0]
        hid = w_in.shape[1]
        taps = math.isqrt(dw_weight.shape[0])
        half = side // 2
        cells = half * half
        chunks = channels // LANES
        assert width == side and llm_peer.shape == (1, 1)
        f32, bf16 = jnp.float32, jnp.bfloat16
        padded = (chunks, side + 2 * (taps // 2), side + 2 * PAD, LANES)
        block = (half, half, channels)
        strip = (half, channels)
        tip = (2, channels)
        hbm = pl.BlockSpec(memory_space=pltpu.HBM)
        pairs = peers // 2
        assert peers == 2 * pairs and pairs > 1
        vmem = pl.BlockSpec(memory_space=pltpu.VMEM)

        def dma(count):
            return pltpu.SemaphoreType.DMA((count,))

        def buf(*shape, kind=f32):
            return pltpu.VMEM(shape, kind)

        inputs = (
            "image_hbm", "owner_hbm", "x_hbm", "tg_hbm", "dww_hbm", "dwb_hbm", "gain_hbm", "lnb_hbm",
            "win_hbm", "bin_hbm", "wout_hbm", "bout_hbm", "scale_hbm", "cw_hbm", "cb_hbm",
        )
        held = {
            "obuf": buf(chunks, side, side, LANES),
            "tokout": buf(slots, *block),
        }
        scratch = {
            "xpad": buf(*padded),
            "gpad": buf(*padded),
            "dww": buf(chunks, taps * taps, LANES),
            "gq": buf(chunks, half, half, LANES),
            "dwb": buf(channels),
            "gain": buf(channels),
            "lnb": buf(channels),
            "bout": buf(channels),
            "scale": buf(channels),
            "cb": buf(channels),
            "bin_": buf(hid),
            "win": buf(*w_in.shape, kind=bf16),
            "wout": buf(*w_out.shape, kind=bf16),
            "cw": buf(*comp_weight.shape, kind=bf16),
            "tg": buf(slots, *block),
            "ntg": buf(slots, *block),
            "sp": buf(chunks, 4, cells, LANES),
            "rstd": buf(4, cells, LANES),
            "nb": buf(4 * cells, channels, kind=bf16),
            "dg": buf(4 * cells, hid),
            "hb": buf(cells, hid, kind=bf16),
            "dpb": buf(4 * cells, hid, kind=bf16),
            "table": buf(peers, 8, LANES, kind=jnp.int32),
            "gmain": buf(pairs, *block),
            "gcols": buf(pairs, 2, *strip),
            "gcorn": buf(pairs, 2, *tip),
            "rmain": buf(pairs - 1, *block),
            "rcols": buf(pairs - 1, 2, *strip),
            "grow": buf(2, pairs, *strip),
            "gcorn_in": buf(2, pairs, *tip),
            "grid_g": buf(half + 2, half + 2 * PAD, channels),
            "grid_p": buf(half + 4, half + 2 * PAD, channels),
            "erow": buf(2, *strip),
            "ecorn": buf(2, *tip),
            "amain": buf(peers, *block),
            "acols": buf(peers, 2, *strip),
            "arow": buf(2, peers, *strip),
            "acorn": buf(2, peers, *tip),
            "image_ref": pltpu.SMEM(image_of_row.shape, jnp.int32),
            "owner_ref": pltpu.SMEM((1, 1), jnp.int32),
            "in_sems": dma(2 * chunks + 13),
        }
        for name, count in (
            ("tab", peers - 1), ("near", 1), ("row", 2 * pairs), ("cor", 2 * pairs), ("far", 2 * pairs - 2),
            ("trow", 2 * pairs), ("tcor", 2 * pairs), ("tok", 2 * pairs), ("pass", 2 * pairs - 2),
            ("prow", 2 * pairs), ("pcor", 2 * pairs),
        ):
            scratch[name + "_send"] = dma(count)
            scratch[name + "_recv"] = dma(count)
        names = inputs + tuple(held) + tuple(scratch)
        state = pl.pallas_call(
            functools.partial(kernel, groups, peers, taps, names),
            out_shape=tuple(held.values()),
            in_specs=[hbm] * len(inputs),
            out_specs=(vmem,) * len(held),
            scratch_shapes=list(scratch.values()),
            compiler_params=pltpu.CompilerParams(collective_id=0, has_side_effects=True),
        )(
            image_of_row,
            llm_peer,
            features,
            token_grads.reshape((slots,) + block),
            dw_weight,
            dw_bias,
            ln_gain,
            ln_bias,
            w_in,
            b_in,
            w_out,
            b_out,
            layer_scale,
            comp_weight,
            comp_bias,
        )
        tokens, grads = pl.pallas_call(
            tail,
            out_shape=(
                jax.ShapeDtypeStruct((slots,) + block, f32),
                jax.ShapeDtypeStruct(features.shape, f32),
            ),
            in_specs=[vmem] * len(held),
            out_specs=(hbm, hbm),
            scratch_shapes=[dma(chunks + 1)],
            compiler_params=pltpu.CompilerParams(vmem_limit_bytes=16 << 20),
        )(*state)
        return tokens.reshape(slots, cells, channels), grads

    placed = [P()] * 15
    placed[0] = P("group", "peer", None)
    placed[2] = P(("group", "peer"), None)
    placed[3] = P(("group", "peer"), None, None)
    return jax.shard_map(
        on_device,
        mesh=mesh,
        in_specs=tuple(placed),
        out_specs=(P(("group", "peer"), None, None), P("group", "peer", None)),
        check_vma=False,
    )
```

time: 24.6 us -> 20.5 us (0.83)
  the two profiles are of different devices: /device:TPU:1 before, /device:TPU:0 now
where the time goes in v1:
time: 20.5 us; the launch traced here: 20.3 us
  Pallas kernels  19 us (93%)
  between operations  1.29 us (6%)
    pallas_call x1, Pallas kernels, on_device(): pl.pallas_call(functools.partial(kernel, groups, peers, taps, names), out...  18.2 us
    pallas_call x1, Pallas kernels, on_device(): pl.pallas_call(tail, out_shape=(jax.ShapeDtypeStruct((slots,) + block, f3...  0.84 us

profile of v1, /device:TPU:0, one launch (start us, length us, event | category | flops | bytes accessed | tf_op | source)
XLA Modules:
  0.0 20.3 jit_solution(11975891468022020774)
XLA Ops:
  1.3 18.2 %shard_map.158 = (f32[3,16,16,128]{3,2,1,0:T(8,128)S(1)}, f32[2,8,8,384]{3,2,1,0:T(8,128)S(1)}) custom-call(s32[8]{0:T(128)} %refs_0_.1, s32[1,1]{1,0:T(1,128)S(6)} %copy.17.refs_1_, f32[16,16,384]{2,1,0:T(8,128)} %refs_2_.1, f32[2,8,8,384]{3,2,1,0:T(8,128)} %bitcast.2, f32[49,384]{1,0:T(8,128)} %refs_4_.1, f32[384]{0:T(512)} %refs_5_.1, f32[384]{0:T(512)} %refs_6_.1, ...), custom_call_target="tpu_custom_call" | custom-call | tf_op jit(solution)/shard_map/pallas_call | solution.py:574
  19.5 0.8 %shard_map.159 = (f32[2,8,8,384]{3,2,1,0:T(8,128)}, f32[16,16,384]{2,1,0:T(8,128)}) custom-call(f32[3,16,16,128]{3,2,1,0:T(8,128)S(1)} %get-tuple-element.6.obuf, f32[2,8,8,384]{3,2,1,0:T(8,128)S(1)} %get-tuple-element.7.tokout), custom_call_target="tpu_custom_call" | custom-call | tf_op jit(solution)/shard_map/pallas_call | solution.py:598

commit v2 on v1

--- a/solution.py
+++ b/solution.py
@@ -14,6 +14,8 @@
 PAD = 8
 BLOCK = 256
 WIDE = 16
+TABLE, NEAR, GROWS, GFAR, TROWS, TFAR, TNEAR, PASS, PROWS = 0, 1, 2, 4, 5, 7, 8, 9, 10
+SENT_BY = (0, 0, 1, 2, 0, 1, 2, 0, 0, 0, 3, 4)
 
 
 def nt_dot(a, b):
@@ -51,7 +53,6 @@
     pairs = peers // 2
     core = lax.rem(me, 2)
     partner = me + 1 - 2 * core
-    small = (r.dwb, r.gain, r.lnb, r.bout, r.scale, r.cb)
     inner = slice(PAD, PAD + half)
 
     def vector(ref, lane=slice(None)):
@@ -75,29 +76,49 @@
 
         @pl.when(beyond[dr])
         def _():
-            for k in range(pairs):
-                greet(g + dr, seat(k, core))
+            greet(g + dr, me)
 
     copies = {}
 
-    def fetch(name, src, dst):
-        copy = pltpu.make_async_copy(src, dst, r.in_sems.at[len(copies)])
-        copy.start()
-        copies[name] = copy
-
-    fetch("owner", r.owner_hbm, r.owner_ref)
-    fetch("tg", r.tg_hbm, r.tg)
+    def fetch(name, *moves):
+        sem = r.in_sems.at[len(copies)]
+        copies[name] = [pltpu.make_async_copy(src, dst, sem) for src, dst in moves]
+        for copy in copies[name]:
+            copy.start()
+
+    def settle(sem, elements):
+        span = r.span.at[pl.ds(0, elements // LANES)]
+        pltpu.make_async_copy(span, span, sem).wait()
+
+    def fetched(name):
+        if len(copies[name]) == 1:
+            copies[name][0].wait()
+        else:
+            elements = sum(math.prod(copy.dst_ref.shape) for copy in copies[name])
+            settle(r.in_sems.at[list(copies).index(name)], elements)
+
+    fetch("owner", (r.owner_hbm, r.owner_ref))
+    fetch("tg", (r.tg_hbm, r.tg))
+    fetch(
+        "small",
+        (r.dwb_hbm, r.dwb),
+        (r.gain_hbm, r.gain),
+        (r.lnb_hbm, r.lnb),
+        (r.bout_hbm, r.bout),
+        (r.scale_hbm, r.scale),
+        (r.cb_hbm, r.cb),
+        (r.bin_hbm, r.bin_),
+    )
+    by_lane = []
     for c in range(chunks):
         lane = slice(c * LANES, (c + 1) * LANES)
-        fetch(("w", c), r.dww_hbm.at[:, lane], r.dww.at[c])
-        fetch(("x", c), r.x_hbm.at[:, :, lane], r.xpad.at[c, reach : reach + side, PAD : PAD + side, :])
-    for i, src in enumerate((r.dwb_hbm, r.gain_hbm, r.lnb_hbm, r.bout_hbm, r.scale_hbm, r.cb_hbm)):
-        fetch(("s", i), src, small[i])
-    fetch("image", r.image_hbm, r.image_ref)
-    fetch("bin", r.bin_hbm, r.bin_)
-    fetch("win", r.win_hbm, r.win)
-    fetch("wout", r.wout_hbm, r.wout)
-    fetch("cw", r.cw_hbm, r.cw)
+        by_lane.append((r.dww_hbm.at[:, lane], r.dww.at[c]))
+        by_lane.append((r.x_hbm.at[:, :, lane], r.xpad.at[c, reach : reach + side, PAD : PAD + side, :]))
+    fetch("x", *by_lane)
+    fetch("image", (r.image_hbm, r.image_ref))
+    fetch("win", (r.win_hbm, r.win))
+    fetch("wout", (r.wout_hbm, r.wout))
+    fetch("cw", (r.cw_hbm, r.cw))
 
     def clear(buf):
         width = buf.shape[2]
@@ -111,48 +132,48 @@
     clear(r.gpad)
     r.grid_p[...] = jnp.zeros_like(r.grid_p)
 
-    def move(src, dst, sems, index, where, row=None):
-        send, recv = sems
+    def move(src, dst, group, where, row=None):
         return pltpu.make_async_remote_copy(
             src_ref=src,
             dst_ref=dst,
-            send_sem=send.at[index],
-            recv_sem=recv.at[index],
+            send_sem=r.send.at[SENT_BY[group]],
+            recv_sem=r.recv.at[group],
             device_id={"group": g if row is None else row, "peer": where},
             device_id_type=MESH,
         )
 
-    copies["owner"].wait()
+    fetched("owner")
     r.table[me] = jnp.full((8, LANES), r.owner_ref[0, 0], jnp.int32)
     along = (g > 0).astype(jnp.int32) + (g < groups - 1).astype(jnp.int32)
-    pl.semaphore_wait(barrier, peers - 1 + pairs * along)
-
-    tab_sems = (r.tab_send, r.tab_recv)
+    pl.semaphore_wait(barrier, peers - 1 + along)
+
     table_moves = [
-        move(r.table.at[me], r.table.at[me], tab_sems, k - 1, lax.rem(me + k, peers)) for k in range(1, peers)
+        move(r.table.at[me], r.table.at[me], TABLE, lax.rem(me + k, peers)) for k in range(1, peers)
     ]
     for m in table_moves:
         m.start()
-    copies["tg"].wait()
-    near_move = move(r.tg, r.ntg, (r.near_send, r.near_recv), 0, partner)
+    fetched("tg")
+    near_move = move(r.tg, r.ntg, NEAR, partner)
     near_move.start()
 
     def forward_conv(c):
         outs = depthwise(r.xpad, r.dww, c, taps, side, False)
-        bias = vector(small[0], slice(c * LANES, (c + 1) * LANES))
+        bias = vector(r.dwb, slice(c * LANES, (c + 1) * LANES))
         for parity in range(2):
             part = (outs[parity] + bias).reshape(half, 2, half, LANES)
             for row in range(2):
                 r.sp[c, row * 2 + parity] = part[:, row].reshape(cells, LANES)
 
-    copies[("s", 0)].wait()
+    fetched("small")
+    fetched("x")
     for c in range(chunks):
-        copies[("w", c)].wait()
-        copies[("x", c)].wait()
         forward_conv(c)
-    for m in table_moves:
-        m.wait()
-    near_move.wait()
+    tile = cells * channels
+    edge = half * channels
+    main = (pairs - 1) * (tile + 2 * edge)
+    strips = pairs * (edge + 2 * channels)
+    settle(r.recv.at[TABLE], (peers - 1) * 8 * LANES)
+    settle(r.recv.at[NEAR], slots * tile)
 
     def masks_of(who, device):
         inside = jnp.logical_and(who >= 0, who < peers)
@@ -188,16 +209,13 @@
             r.gcorn[k, d, 0:1, :] = left[at : at + 1]
             r.gcorn[k, d, 1:2, :] = right[at : at + 1]
 
-    row_sems = (r.row_send, r.row_recv)
-    cor_sems = (r.cor_send, r.cor_recv)
-
-    def row_moves(src_row, src_corner, dst_row, dst_corner, sems_r, sems_c):
+    def row_moves(src_row, src_corner, dst_row, dst_corner, group, which):
         moves = {}
         for d, dr in ((0, -1), (1, 1)):
             for k in range(pairs):
                 moves[d, k] = (
-                    move(src_row(d, k), dst_row(d, k), sems_r, d * pairs + k, seat(k, core), g + dr),
-                    move(src_corner(d, k), dst_corner(d, k), sems_c, d * pairs + k, seat(k, core), g + dr),
+                    move(src_row(d, k), dst_row(d, k), group + d, seat(k, which), g + dr),
+                    move(src_corner(d, k), dst_corner(d, k), group + d, seat(k, which), g + dr),
                 )
         return moves
 
@@ -210,43 +228,32 @@
                     for m in moves[d, k]:
                         m.start()
 
-    def sent_rows(moves):
-        for d, dr in ((0, -1), (1, 1)):
-
-            @pl.when(beyond[dr])
-            def _():
-                for k in range(pairs):
-                    for m in moves[d, k]:
-                        m.wait_send()
-
-    def received_rows(moves):
+    def received_rows(group):
         for d, dr in ((0, -1), (1, 1)):
 
             @pl.when(beyond[-dr])
             def _():
-                for k in range(pairs):
-                    for m in moves[d, k]:
-                        m.wait_recv()
+                settle(r.recv.at[group + d], strips)
 
     g_rows = row_moves(
         lambda d, k: r.gmain.at[k, 0 if d == 0 else half - 1],
         lambda d, k: r.gcorn.at[k, d],
         lambda d, k: r.grow.at[d, k],
         lambda d, k: r.gcorn_in.at[d, k],
-        row_sems,
-        cor_sems,
+        GROWS,
+        core,
     )
     start_rows(g_rows)
-    far_sems = (r.far_send, r.far_recv)
     g_far = []
     for k in range(1, pairs):
-        g_far.append(move(r.gcols.at[k], r.rcols.at[k - 1], far_sems, 2 * k - 2, seat(k, core)))
-        g_far.append(move(r.gmain.at[k], r.rmain.at[k - 1], far_sems, 2 * k - 1, seat(k, core)))
-    for m in g_far:
-        m.start()
-
-    for i in range(1, 6):
-        copies[("s", i)].wait()
+        g_far.append(move(r.gcols.at[k], r.rcols.at[k - 1], GFAR, seat(k, core)))
+        g_far.append(move(r.gmain.at[k], r.rmain.at[k - 1], GFAR, seat(k, core)))
+
+    @pl.when(core == 0)
+    def _():
+        for m in g_far:
+            m.start()
+
     for q in range(4):
         parts = [r.sp[c, q] for c in range(chunks)]
         mean = jnp.sum(functools.reduce(jnp.add, parts), axis=1, keepdims=True) / channels
@@ -259,12 +266,10 @@
             hat = parts[c] * inv
             r.sp[c, q] = hat
             r.nb[q * cells : (q + 1) * cells, lane] = (
-                hat * vector(small[1], lane) + vector(small[2], lane)
+                hat * vector(r.gain, lane) + vector(r.lnb, lane)
             ).astype(jnp.bfloat16)
 
-    copies["bin"].wait()
-    copies["image"].wait()
-    copies["win"].wait()
+    fetched("win")
     for n in range(hid // BLOCK):
         lane = slice(n * BLOCK, (n + 1) * BLOCK)
         pre_all = jnp.dot(r.nb[...], r.win[:, lane], preferred_element_type=jnp.float32)
@@ -278,7 +283,12 @@
             value = pre * cdf
             pooled = value if pooled is None else pooled + value
         r.hb[:, lane] = (pooled * 0.25).astype(jnp.bfloat16)
-    copies["wout"].wait()
+    @pl.when(core == 1)
+    def _():
+        for m in g_far:
+            m.start()
+
+    fetched("wout")
     branch = jnp.dot(r.hb[...], r.wout[...], preferred_element_type=jnp.float32)
     for c in range(chunks):
         lane = slice(c * LANES, (c + 1) * LANES)
@@ -288,10 +298,10 @@
                 part = r.xpad[c, reach : reach + side, pl.ds(PAD + parity, half, stride=2), :]
                 part = part.reshape(half, 2, half, LANES)[:, row]
                 total = part if total is None else total + part
-        mixed = vector(small[4], lane) * (branch[:, lane] + vector(small[3], lane))
+        mixed = vector(r.scale, lane) * (branch[:, lane] + vector(r.bout, lane))
         r.grid_p[2 : half + 2, inner, lane] = total * 0.25 + mixed.reshape(half, half, LANES)
 
-    copies["cw"].wait()
+    fetched("cw")
     rim = half + 2
     comp = None
     for a in range(3):
@@ -308,38 +318,35 @@
         r.ecorn[d, 0:1, :] = comp[at, 0:1]
         r.ecorn[d, 1:2, :] = comp[at, half + 1 : half + 2]
 
-    trow_sems = (r.trow_send, r.trow_recv)
-    tcor_sems = (r.tcor_send, r.tcor_recv)
     t_rows = row_moves(
         lambda d, k: r.erow.at[d],
         lambda d, k: r.ecorn.at[d],
         lambda d, k: r.arow.at[d, me],
         lambda d, k: r.acorn.at[d, me],
-        trow_sems,
-        tcor_sems,
+        TROWS,
+        1 - core,
     )
     start_rows(t_rows)
-    tok_sems = (r.tok_send, r.tok_recv)
     t_far = []
     for k in range(1, pairs):
-        t_far.append(move(r.acols.at[me], r.acols.at[me], tok_sems, 2 * k, seat(k, core)))
-        t_far.append(move(r.amain.at[me], r.amain.at[me], tok_sems, 2 * k + 1, seat(k, core)))
+        t_far.append(move(r.acols.at[me], r.acols.at[me], TFAR, seat(k, 1 - core)))
+        t_far.append(move(r.amain.at[me], r.amain.at[me], TFAR, seat(k, 1 - core)))
     t_near = [
-        move(r.acols.at[me], r.acols.at[me], tok_sems, 0, partner),
-        move(r.amain.at[me], r.amain.at[me], tok_sems, 1, partner),
+        move(r.acols.at[me], r.acols.at[me], TNEAR, partner),
+        move(r.amain.at[me], r.amain.at[me], TNEAR, partner),
     ]
     for m in t_far + t_near:
         m.start()
 
+    fetched("image")
     image = r.image_ref[g]
     keep = {}
     for d, near in ((1, jnp.maximum(g - 1, 0)), (0, jnp.minimum(g + 1, groups - 1))):
         there = (g > 0) if d == 1 else (g < groups - 1)
         keep[d] = (r.image_ref[near] == image).astype(jnp.float32) * there.astype(jnp.float32)
 
-    received_rows(g_rows)
-    for m in g_far:
-        m.wait_recv()
+    received_rows(GROWS)
+    settle(r.recv.at[GFAR], main)
     def far(own, other):
         return total_of([own] + [other(k) for k in range(pairs - 1)])
     r.grid_g[1 : half + 1, inner, :] = far(r.gmain[0], lambda k: r.rmain[k])
@@ -394,27 +401,24 @@
     for c in range(chunks - 1):
         backward_conv(c)
 
-    received_rows(t_rows)
-    for m in t_far:
-        m.wait_recv()
-    pass_sems = (r.pass_send, r.pass_recv)
+    received_rows(TROWS)
+    settle(r.recv.at[TFAR], main)
     passed = []
     for k in range(1, pairs):
-        who = seat(pairs - k, core)
-        passed.append(move(r.acols.at[who], r.acols.at[who], pass_sems, 2 * k - 2, partner))
-        passed.append(move(r.amain.at[who], r.amain.at[who], pass_sems, 2 * k - 1, partner))
+        who = seat(k, 1 - core)
+        passed.append(move(r.acols.at[who], r.acols.at[who], PASS, partner))
+        passed.append(move(r.amain.at[who], r.amain.at[who], PASS, partner))
     for m in passed:
         m.start()
-    prow_sems = (r.prow_send, r.prow_recv)
-    pcor_sems = (r.pcor_send, r.pcor_recv)
     passed_rows = {}
     for d, dr in ((0, -1), (1, 1)):
         for k in range(pairs):
-            who = seat(k, core)
+            who = seat(k, 1 - core)
             passed_rows[d, k] = (
-                move(r.arow.at[d, who], r.arow.at[d, who], prow_sems, d * pairs + k, partner),
-                move(r.acorn.at[d, who], r.acorn.at[d, who], pcor_sems, d * pairs + k, partner),
+                move(r.arow.at[d, who], r.arow.at[d, who], PROWS + d, partner),
+                move(r.acorn.at[d, who], r.acorn.at[d, who], PROWS + d, partner),
             )
+
         @pl.when(beyond[-dr])
         def _():
             for k in range(pairs):
@@ -423,19 +427,20 @@
 
     backward_conv(chunks - 1)
 
-    for m in t_near + passed:
-        m.wait()
-    for m in t_far + g_far:
-        m.wait_send()
-    sent_rows(g_rows)
-    sent_rows(t_rows)
+    settle(r.recv.at[TNEAR], tile + 2 * edge)
+    settle(r.recv.at[PASS], main)
+    received_rows(PROWS)
+
+    settle(r.send.at[0], (peers - 1) * 8 * LANES + slots * tile + 3 * main + tile + 2 * edge)
     for d, dr in ((0, -1), (1, 1)):
+
+        @pl.when(beyond[dr])
+        def _():
+            settle(r.send.at[1 + d], 2 * strips)
 
         @pl.when(beyond[-dr])
         def _():
-            for k in range(pairs):
-                for m in passed_rows[d, k]:
-                    m.wait()
+            settle(r.send.at[3 + d], strips)
 
     chosen = [[wide(mask) for mask in masks_of(p, me)] for p in range(peers)]
     bias = vector(r.cb)
@@ -520,6 +525,9 @@
             "obuf": buf(chunks, side, side, LANES),
             "tokout": buf(slots, *block),
         }
+        sent = (slots + 1) * cells * channels + 2 * half * channels + peers * 8 * LANES
+        sent += 3 * (pairs - 1) * (cells + 2 * half) * channels
+        span = max(sent, (side * side + taps * taps) * channels) // LANES
         scratch = {
             "xpad": buf(*padded),
             "gpad": buf(*padded),
@@ -561,15 +569,11 @@
             "acorn": buf(2, peers, *tip),
             "image_ref": pltpu.SMEM(image_of_row.shape, jnp.int32),
             "owner_ref": pltpu.SMEM((1, 1), jnp.int32),
-            "in_sems": dma(2 * chunks + 13),
+            "in_sems": dma(8),
+            "send": dma(5),
+            "span": buf(span, 1, LANES),
+            "recv": dma(12),
         }
-        for name, count in (
-            ("tab", peers - 1), ("near", 1), ("row", 2 * pairs), ("cor", 2 * pairs), ("far", 2 * pairs - 2),
-            ("trow", 2 * pairs), ("tcor", 2 * pairs), ("tok", 2 * pairs), ("pass", 2 * pairs - 2),
-            ("prow", 2 * pairs), ("pcor", 2 * pairs),
-        ):
-            scratch[name + "_send"] = dma(count)
-            scratch[name + "_recv"] = dma(count)
         names = inputs + tuple(held) + tuple(scratch)
         state = pl.pallas_call(
             functools.partial(kernel, groups, peers, taps, names),

time: 20.5 us -> 19.3 us (0.941)
  Pallas kernels: 19 us -> 17.9 us
    pallas_call x1, Pallas kernels: 18.2 us -> 17 us  [on_device(): pl.pallas_call(functools.partial(kernel, groups, peers, taps, names), out...]
where the time goes in v2:
time: 19.3 us; the launch traced here: 19.2 us
  Pallas kernels  17.9 us (93%)
  between operations  1.29 us (7%)
    pallas_call x1, Pallas kernels, on_device(): pl.pallas_call(functools.partial(kernel, groups, peers, taps, names), out...  17 us
    pallas_call x1, Pallas kernels, on_device(): pl.pallas_call(tail, out_shape=(jax.ShapeDtypeStruct((slots,) + block, f3...  0.84 us

profile of v2, /device:TPU:0, one launch (start us, length us, event | category | flops | bytes accessed | tf_op | source)
XLA Modules:
  0.0 19.2 jit_solution(2503856351005488337)
XLA Ops:
  1.3 17.0 %shard_map.158 = (f32[3,16,16,128]{3,2,1,0:T(8,128)S(1)}, f32[2,8,8,384]{3,2,1,0:T(8,128)S(1)}) custom-call(s32[8]{0:T(128)} %refs_0_.1, s32[1,1]{1,0:T(1,128)S(6)} %copy.17.refs_1_, f32[16,16,384]{2,1,0:T(8,128)} %refs_2_.1, f32[2,8,8,384]{3,2,1,0:T(8,128)} %bitcast.2, f32[49,384]{1,0:T(8,128)} %refs_4_.1, f32[384]{0:T(512)} %refs_5_.1, f32[384]{0:T(512)} %refs_6_.1, ...), custom_call_target="tpu_custom_call" | custom-call | tf_op jit(solution)/shard_map/pallas_call | solution.py:578
  18.3 0.8 %shard_map.159 = (f32[2,8,8,384]{3,2,1,0:T(8,128)}, f32[16,16,384]{2,1,0:T(8,128)}) custom-call(f32[3,16,16,128]{3,2,1,0:T(8,128)S(1)} %get-tuple-element.6.obuf, f32[2,8,8,384]{3,2,1,0:T(8,128)S(1)} %get-tuple-element.7.tokout), custom_call_target="tpu_custom_call" | custom-call | tf_op jit(solution)/shard_map/pallas_call | solution.py:602

commit v3 on v2

--- a/solution.py
+++ b/solution.py
@@ -14,8 +14,8 @@
 PAD = 8
 BLOCK = 256
 WIDE = 16
-TABLE, NEAR, GROWS, GFAR, TROWS, TFAR, TNEAR, PASS, PROWS = 0, 1, 2, 4, 5, 7, 8, 9, 10
-SENT_BY = (0, 0, 1, 2, 0, 1, 2, 0, 0, 0, 3, 4)
+TABLE, NEAR, GROWS, GFAR, TROWS, TFAR, TNEAR, PASS, PROWS, RAW, RELAY = 0, 1, 2, 4, 5, 7, 8, 9, 10, 12, 13
+SENT_BY = (0, 0, 1, 2, 0, 1, 2, 0, 0, 0, 3, 4, 0, 0)
 
 
 def nt_dot(a, b):
@@ -72,11 +72,9 @@
 
     for k in range(1, peers):
         greet(g, lax.rem(me + k, peers))
-    for dr in (-1, 1):
-
-        @pl.when(beyond[dr])
-        def _():
-            greet(g + dr, me)
+    @pl.when(beyond[1])
+    def _():
+        greet(g + 1, me)
 
     copies = {}
 
@@ -144,8 +142,12 @@
 
     fetched("owner")
     r.table[me] = jnp.full((8, LANES), r.owner_ref[0, 0], jnp.int32)
-    along = (g > 0).astype(jnp.int32) + (g < groups - 1).astype(jnp.int32)
-    pl.semaphore_wait(barrier, peers - 1 + along)
+    pl.semaphore_wait(barrier, peers - 1 + (g > 0).astype(jnp.int32))
+
+    @pl.when(beyond[-1])
+    def _():
+        pl.semaphore_signal(r.hello, inc=1, device_id={"group": g - 1, "peer": me}, device_id_type=MESH)
+
 
     table_moves = [
         move(r.table.at[me], r.table.at[me], TABLE, lax.rem(me + k, peers)) for k in range(1, peers)
@@ -155,6 +157,10 @@
     fetched("tg")
     near_move = move(r.tg, r.ntg, NEAR, partner)
     near_move.start()
+    upper = half // 2
+    raw_moves = [move(r.tg.at[:, upper:], r.xtg.at[0, k - 1], RAW, seat(k, core)) for k in range(1, pairs)]
+    for m in raw_moves:
+        m.start()
 
     def forward_conv(c):
         outs = depthwise(r.xpad, r.dww, c, taps, side, False)
@@ -171,89 +177,9 @@
     tile = cells * channels
     edge = half * channels
     main = (pairs - 1) * (tile + 2 * edge)
+    masked = (pairs - 1) * upper * 2 * (edge // 2 + channels)
+    raw = (pairs - 1) * slots * (half - upper) * edge
     strips = pairs * (edge + 2 * channels)
-    settle(r.recv.at[TABLE], (peers - 1) * 8 * LANES)
-    settle(r.recv.at[NEAR], slots * tile)
-
-    def masks_of(who, device):
-        inside = jnp.logical_and(who >= 0, who < peers)
-        at = jnp.clip(who, 0, peers - 1)
-        mine = jnp.logical_and(r.table[at] == device, inside)
-        before = jnp.zeros((8, LANES), jnp.int32)
-        for p in range(peers):
-            earlier = (p < at).astype(jnp.int32)
-            before = before + jnp.where(r.table[p] == device, earlier, 0)
-        return [jnp.logical_and(mine, before == s).astype(jnp.float32) for s in range(slots)]
-
-    def wide(mask):
-        return jnp.concatenate([mask] * chunks, axis=1)
-
-    def held(who):
-        pairs_of = []
-        for ref, device in ((r.tg, me), (r.ntg, partner)):
-            for s, mask in enumerate(masks_of(who, device)):
-                pairs_of.append((ref, s, wide(mask)))
-        return pairs_of
-
-    def total_of(terms):
-        return functools.reduce(jnp.add, terms)
-
-    for k in range(pairs):
-        home = seat(k, core)
-        r.gmain[k] = total_of([ref[s] * mask for ref, s, mask in held(home)])
-        left = total_of([ref[s, :, half - 1, :] * mask for ref, s, mask in held(home - 1)])
-        right = total_of([ref[s, :, 0, :] * mask for ref, s, mask in held(home + 1)])
-        r.gcols[k, 0] = left
-        r.gcols[k, 1] = right
-        for d, at in ((0, 0), (1, half - 1)):
-            r.gcorn[k, d, 0:1, :] = left[at : at + 1]
-            r.gcorn[k, d, 1:2, :] = right[at : at + 1]
-
-    def row_moves(src_row, src_corner, dst_row, dst_corner, group, which):
-        moves = {}
-        for d, dr in ((0, -1), (1, 1)):
-            for k in range(pairs):
-                moves[d, k] = (
-                    move(src_row(d, k), dst_row(d, k), group + d, seat(k, which), g + dr),
-                    move(src_corner(d, k), dst_corner(d, k), group + d, seat(k, which), g + dr),
-                )
-        return moves
-
-    def start_rows(moves):
-        for d, dr in ((0, -1), (1, 1)):
-
-            @pl.when(beyond[dr])
-            def _():
-                for k in reversed(range(pairs)):
-                    for m in moves[d, k]:
-                        m.start()
-
-    def received_rows(group):
-        for d, dr in ((0, -1), (1, 1)):
-
-            @pl.when(beyond[-dr])
-            def _():
-                settle(r.recv.at[group + d], strips)
-
-    g_rows = row_moves(
-        lambda d, k: r.gmain.at[k, 0 if d == 0 else half - 1],
-        lambda d, k: r.gcorn.at[k, d],
-        lambda d, k: r.grow.at[d, k],
-        lambda d, k: r.gcorn_in.at[d, k],
-        GROWS,
-        core,
-    )
-    start_rows(g_rows)
-    g_far = []
-    for k in range(1, pairs):
-        g_far.append(move(r.gcols.at[k], r.rcols.at[k - 1], GFAR, seat(k, core)))
-        g_far.append(move(r.gmain.at[k], r.rmain.at[k - 1], GFAR, seat(k, core)))
-
-    @pl.when(core == 0)
-    def _():
-        for m in g_far:
-            m.start()
-
     for q in range(4):
         parts = [r.sp[c, q] for c in range(chunks)]
         mean = jnp.sum(functools.reduce(jnp.add, parts), axis=1, keepdims=True) / channels
@@ -269,6 +195,102 @@
                 hat * vector(r.gain, lane) + vector(r.lnb, lane)
             ).astype(jnp.bfloat16)
 
+    settle(r.recv.at[TABLE], (peers - 1) * 8 * LANES)
+    settle(r.recv.at[NEAR], slots * tile)
+
+    def masks_of(who, device):
+        inside = jnp.logical_and(who >= 0, who < peers)
+        at = jnp.clip(who, 0, peers - 1)
+        mine = jnp.logical_and(r.table[at] == device, inside)
+        before = jnp.zeros((8, LANES), jnp.int32)
+        for p in range(peers):
+            earlier = (p < at).astype(jnp.int32)
+            before = before + jnp.where(r.table[p] == device, earlier, 0)
+        return [jnp.logical_and(mine, before == s).astype(jnp.float32) for s in range(slots)]
+
+    def wide(mask):
+        return jnp.concatenate([mask] * chunks, axis=1)
+
+    def held(who):
+        pairs_of = []
+        for ref, device in ((r.tg, me), (r.ntg, partner)):
+            for s, mask in enumerate(masks_of(who, device)):
+                pairs_of.append((ref.at[s], wide(mask)))
+        return pairs_of
+
+    def held_far(who):
+        pairs_of = []
+        for k in range(1, pairs):
+            for via, which in ((0, core), (1, 1 - core)):
+                for s, mask in enumerate(masks_of(who, seat(pairs - k, which))):
+                    pairs_of.append((r.xtg.at[via, k - 1, s], wide(mask)))
+        return pairs_of
+
+    def total_of(terms):
+        return functools.reduce(jnp.add, terms)
+
+    for k in range(pairs):
+        home = seat(k, core)
+        whole = held(home)
+        for part in ((slice(0, half),) if k == 0 else (slice(0, upper), slice(half - 1, half))):
+            r.gmain[k, part] = total_of([ref[part] * mask for ref, mask in whole])
+        left = total_of([ref[:, half - 1, :] * mask for ref, mask in held(home - 1)])
+        right = total_of([ref[:, 0, :] * mask for ref, mask in held(home + 1)])
+        for side_at, col in ((0, left), (1, right)):
+            if k == 0:
+                r.gcols[side_at] = col
+            else:
+                r.gfar[k - 1, side_at] = col[:upper]
+            for d, at in ((0, 0), (1, half - 1)):
+                r.gcorn[k, d, side_at : side_at + 1, :] = col[at : at + 1]
+
+    def row_moves(src_row, src_corner, dst_row, dst_corner, group, which):
+        moves = {}
+        for d, dr in ((0, -1), (1, 1)):
+            for k in range(pairs):
+                moves[d, k] = (
+                    move(src_row(d, k), dst_row(d, k), group + d, seat(k, which), g + dr),
+                    move(src_corner(d, k), dst_corner(d, k), group + d, seat(k, which), g + dr),
+                )
+        return moves
+
+    def start_rows(moves):
+        for d, dr in ((0, -1), (1, 1)):
+
+            @pl.when(beyond[dr])
+            def _():
+                for k in reversed(range(pairs)):
+                    for m in moves[d, k]:
+                        m.start()
+
+    def received_rows(group):
+        for d, dr in ((0, -1), (1, 1)):
+
+            @pl.when(beyond[-dr])
+            def _():
+                settle(r.recv.at[group + d], strips)
+
+    g_rows = row_moves(
+        lambda d, k: r.gmain.at[k, 0 if d == 0 else half - 1],
+        lambda d, k: r.gcorn.at[k, d],
+        lambda d, k: r.grow.at[d, k],
+        lambda d, k: r.gcorn_in.at[d, k],
+        GROWS,
+        core,
+    )
+    @pl.when(beyond[1])
+    def _():
+        pl.semaphore_wait(r.hello, 1)
+
+    start_rows(g_rows)
+    g_far = []
+    for k in range(1, pairs):
+        g_far.append(move(r.gfar.at[k - 1], r.rcols.at[k - 1], GFAR, seat(k, core)))
+        g_far.append(move(r.gmain.at[k, :upper], r.rmain.at[k - 1], GFAR, seat(k, core)))
+
+    for m in g_far:
+        m.start()
+
     fetched("win")
     for n in range(hid // BLOCK):
         lane = slice(n * BLOCK, (n + 1) * BLOCK)
@@ -283,11 +305,6 @@
             value = pre * cdf
             pooled = value if pooled is None else pooled + value
         r.hb[:, lane] = (pooled * 0.25).astype(jnp.bfloat16)
-    @pl.when(core == 1)
-    def _():
-        for m in g_far:
-            m.start()
-
     fetched("wout")
     branch = jnp.dot(r.hb[...], r.wout[...], preferred_element_type=jnp.float32)
     for c in range(chunks):
@@ -301,22 +318,14 @@
         mixed = vector(r.scale, lane) * (branch[:, lane] + vector(r.bout, lane))
         r.grid_p[2 : half + 2, inner, lane] = total * 0.25 + mixed.reshape(half, half, LANES)
 
+    r.grid_p[2 : half + 2, PAD + WIDE, :] = r.grid_p[2 : half + 2, PAD, :]
     fetched("cw")
     rim = half + 2
-    comp = None
     for a in range(3):
         for b in range(3):
-            part = r.grid_p[a : a + rim, PAD - 2 + b : PAD - 2 + b + WIDE, :]
-            part = part.reshape(rim * WIDE, channels).astype(jnp.bfloat16)
-            part = jnp.dot(part, r.cw[a * 3 + b], preferred_element_type=jnp.float32)
-            comp = part if comp is None else comp + part
-    comp = comp.reshape(rim, WIDE, channels)
-    r.amain[me] = comp[1 : half + 1, 1 : half + 1]
-    for d, at in ((0, 0), (1, half + 1)):
-        r.acols[me, d] = comp[1 : half + 1, at]
-        r.erow[d] = comp[at, 1 : half + 1]
-        r.ecorn[d, 0:1, :] = comp[at, 0:1]
-        r.ecorn[d, 1:2, :] = comp[at, half + 1 : half + 2]
+            part = r.grid_p[a : a + rim, PAD - 1 + b : PAD - 1 + b + WIDE, :]
+            at = (a * 3 + b) * channels
+            r.lhs[:, at : at + channels] = part.reshape(rim * WIDE, channels).astype(jnp.bfloat16)
 
     t_rows = row_moves(
         lambda d, k: r.erow.at[d],
@@ -326,17 +335,42 @@
         TROWS,
         1 - core,
     )
-    start_rows(t_rows)
     t_far = []
-    for k in range(1, pairs):
-        t_far.append(move(r.acols.at[me], r.acols.at[me], TFAR, seat(k, 1 - core)))
-        t_far.append(move(r.amain.at[me], r.amain.at[me], TFAR, seat(k, 1 - core)))
+    spans = [slice(at, min(at + 3 * LANES, channels)) for at in range(0, channels, 3 * LANES)]
+    for lane in spans:
+        comp = jnp.dot(r.lhs[...], r.cw[:, lane], preferred_element_type=jnp.float32)
+        comp = comp.reshape(rim, WIDE, -1)
+        r.amain[me, :, :, lane] = comp[1 : half + 1, :half]
+        r.beside[:, :, lane] = comp[:, half:]
+        for d, at, col in ((0, 0, WIDE - 1 - half), (1, half + 1, 0)):
+            r.acols[me, d, :, lane] = r.beside[1 : half + 1, col, lane]
+            r.erow[d, :, lane] = comp[at, :half]
+            r.ecorn[d, 0:1, lane] = r.beside[at, WIDE - 1 - half : WIDE - half, lane]
+            r.ecorn[d, 1:2, lane] = r.beside[at, 0:1, lane]
+        sends = []
+        for k in range(1, pairs):
+            for ref in (r.acols.at[me, :, :, lane], r.amain.at[me, :, :, lane]):
+                sends.append(move(ref, ref, TFAR, seat(k, 1 - core)))
+        if lane is spans[-1]:
+            start_rows(t_rows)
+        for m in sends:
+            m.start()
+        t_far += sends
     t_near = [
         move(r.acols.at[me], r.acols.at[me], TNEAR, partner),
         move(r.amain.at[me], r.amain.at[me], TNEAR, partner),
     ]
-    for m in t_far + t_near:
+    for m in t_near:
         m.start()
+
+    settle(r.recv.at[RAW], raw)
+    relay = move(r.xtg.at[0], r.xtg.at[1], RELAY, partner)
+    relay.start()
+
+    for a in range(3):
+        for b in range(3):
+            at, flipped = (a * 3 + b) * channels, ((2 - a) * 3 + 2 - b) * channels
+            r.cwt[at : at + channels] = r.cw[flipped : flipped + channels].T
 
     fetched("image")
     image = r.image_ref[g]
@@ -345,26 +379,34 @@
         there = (g > 0) if d == 1 else (g < groups - 1)
         keep[d] = (r.image_ref[near] == image).astype(jnp.float32) * there.astype(jnp.float32)
 
+    settle(r.recv.at[RELAY], raw)
+    lower = slice(upper, half)
+    r.grid_g[1 + upper : half + 1, inner, :] = total_of(
+        [r.gmain[0, lower]] + [ref[...] * mask for ref, mask in held_far(me)]
+    )
+    for side_at, who, col, at in ((0, me - 1, half - 1, PAD - 1), (1, me + 1, 0, PAD + half)):
+        r.grid_g[1 + upper : half + 1, at, :] = total_of(
+            [r.gcols[side_at, lower]] + [ref[:, col, :] * mask[: half - upper] for ref, mask in held_far(who)]
+        )
     received_rows(GROWS)
-    settle(r.recv.at[GFAR], main)
-    def far(own, other):
-        return total_of([own] + [other(k) for k in range(pairs - 1)])
-    r.grid_g[1 : half + 1, inner, :] = far(r.gmain[0], lambda k: r.rmain[k])
-    r.grid_g[1 : half + 1, PAD - 1, :] = far(r.gcols[0, 0], lambda k: r.rcols[k, 0])
-    r.grid_g[1 : half + 1, PAD + half, :] = far(r.gcols[0, 1], lambda k: r.rcols[k, 1])
+    settle(r.recv.at[GFAR], masked)
+    r.grid_g[1 : 1 + upper, inner, :] = total_of([r.gmain[0, :upper]] + [r.rmain[k] for k in range(pairs - 1)])
+    for side_at, at in ((0, PAD - 1), (1, PAD + half)):
+        r.grid_g[1 : 1 + upper, at, :] = total_of(
+            [r.gcols[side_at, :upper]] + [r.rcols[k, side_at] for k in range(pairs - 1)]
+        )
     for d, row in ((1, 0), (0, half + 1)):
         r.grid_g[row, inner, :] = total_of([r.grow[d, k] for k in range(pairs)]) * keep[d]
         corner = total_of([r.gcorn_in[d, k] for k in range(pairs)]) * keep[d]
         r.grid_g[row, PAD - 1 : PAD, :] = corner[0:1]
         r.grid_g[row, PAD + half : PAD + half + 1, :] = corner[1:2]
 
-    grads = None
     for a in range(3):
         for b in range(3):
             part = r.grid_g[a : a + half, PAD - 1 + b : PAD - 1 + b + half, :]
-            part = part.reshape(cells, channels).astype(jnp.bfloat16)
-            part = nt_dot(part, r.cw[(2 - a) * 3 + 2 - b])
-            grads = part if grads is None else grads + part
+            at = (a * 3 + b) * channels
+            r.lhs[:cells, at : at + channels] = part.reshape(cells, channels).astype(jnp.bfloat16)
+    grads = jnp.dot(r.lhs[:cells], r.cwt[...], preferred_element_type=jnp.float32)
     grads = grads * 0.25
     for c in range(chunks):
         lane = slice(c * LANES, (c + 1) * LANES)
@@ -398,8 +440,7 @@
             for i in range(side):
                 r.obuf[c, i, pl.ds(parity, half, stride=2), :] = value[i]
 
-    for c in range(chunks - 1):
-        backward_conv(c)
+    backward_conv(0)
 
     received_rows(TROWS)
     settle(r.recv.at[TFAR], main)
@@ -425,13 +466,14 @@
                 for m in passed_rows[d, k]:
                     m.start()
 
-    backward_conv(chunks - 1)
+    for c in range(1, chunks):
+        backward_conv(c)
 
     settle(r.recv.at[TNEAR], tile + 2 * edge)
     settle(r.recv.at[PASS], main)
     received_rows(PROWS)
 
-    settle(r.send.at[0], (peers - 1) * 8 * LANES + slots * tile + 3 * main + tile + 2 * edge)
+    settle(r.send.at[0], (peers - 1) * 8 * LANES + slots * tile + 2 * raw + masked + 2 * main + tile + 2 * edge)
     for d, dr in ((0, -1), (1, 1)):
 
         @pl.when(beyond[dr])
@@ -526,7 +568,7 @@
             "tokout": buf(slots, *block),
         }
         sent = (slots + 1) * cells * channels + 2 * half * channels + peers * 8 * LANES
-        sent += 3 * (pairs - 1) * (cells + 2 * half) * channels
+        sent += (pairs - 1) * (3 * (cells + 2 * half) + 2 * slots * cells) * channels
         span = max(sent, (side * side + taps * taps) * channels) // LANES
         scratch = {
             "xpad": buf(*padded),
@@ -542,7 +584,9 @@
             "bin_": buf(hid),
             "win": buf(*w_in.shape, kind=bf16),
             "wout": buf(*w_out.shape, kind=bf16),
-            "cw": buf(*comp_weight.shape, kind=bf16),
+            "cw": buf(9 * channels, channels, kind=bf16),
+            "cwt": buf(9 * channels, channels, kind=bf16),
+            "lhs": buf((half + 2) * WIDE, 9 * channels, kind=bf16),
             "tg": buf(slots, *block),
             "ntg": buf(slots, *block),
             "sp": buf(chunks, 4, cells, LANES),
@@ -553,14 +597,17 @@
             "dpb": buf(4 * cells, hid, kind=bf16),
             "table": buf(peers, 8, LANES, kind=jnp.int32),
             "gmain": buf(pairs, *block),
-            "gcols": buf(pairs, 2, *strip),
+            "gcols": buf(2, *strip),
+            "gfar": buf(pairs - 1, 2, half // 2, channels),
+            "xtg": buf(2, pairs - 1, slots, half - half // 2, half, channels),
             "gcorn": buf(pairs, 2, *tip),
-            "rmain": buf(pairs - 1, *block),
-            "rcols": buf(pairs - 1, 2, *strip),
+            "rmain": buf(pairs - 1, half // 2, half, channels),
+            "rcols": buf(pairs - 1, 2, half // 2, channels),
             "grow": buf(2, pairs, *strip),
             "gcorn_in": buf(2, pairs, *tip),
             "grid_g": buf(half + 2, half + 2 * PAD, channels),
-            "grid_p": buf(half + 4, half + 2 * PAD, channels),
+            "grid_p": buf(half + 4, PAD + WIDE + PAD, channels),
+            "beside": buf(half + 2, WIDE - half, channels),
             "erow": buf(2, *strip),
             "ecorn": buf(2, *tip),
             "amain": buf(peers, *block),
@@ -570,9 +617,10 @@
             "image_ref": pltpu.SMEM(image_of_row.shape, jnp.int32),
             "owner_ref": pltpu.SMEM((1, 1), jnp.int32),
             "in_sems": dma(8),
+            "hello": pltpu.SemaphoreType.REGULAR,
             "send": dma(5),
             "span": buf(span, 1, LANES),
-            "recv": dma(12),
+            "recv": dma(14),
         }
         names = inputs + tuple(held) + tuple(scratch)
         state = pl.pallas_call(
@@ -596,7 +644,7 @@
             w_out,
             b_out,
             layer_scale,
-            comp_weight,
+            comp_weight.reshape(9 * channels, channels),
             comp_bias,
         )
         tokens, grads = pl.pallas_call(

time: 19.3 us -> 16.7 us (0.87)
  Pallas kernels: 17.9 us -> 15.2 us
    pallas_call x1, Pallas kernels: 17 us -> 14.4 us  [on_device(): pl.pallas_call(functools.partial(kernel, groups, peers, taps, names), out...]
where the time goes in v3:
time: 16.7 us; the launch traced here: 16.5 us
  Pallas kernels  15.2 us (91%)
  between operations  1.29 us (8%)
    pallas_call x1, Pallas kernels, on_device(): pl.pallas_call(functools.partial(kernel, groups, peers, taps, names), out...  14.4 us
    pallas_call x1, Pallas kernels, on_device(): pl.pallas_call(tail, out_shape=(jax.ShapeDtypeStruct((slots,) + block, f3...  0.84 us

profile of v3, /device:TPU:0, one launch (start us, length us, event | category | flops | bytes accessed | tf_op | source)
XLA Modules:
  0.0 16.5 jit_solution(12114625306469269602)
XLA Ops:
  1.3 14.4 %shard_map.158 = (f32[3,16,16,128]{3,2,1,0:T(8,128)S(1)}, f32[2,8,8,384]{3,2,1,0:T(8,128)S(1)}) custom-call(s32[8]{0:T(128)} %refs_0_.1, s32[1,1]{1,0:T(1,128)S(6)} %copy.17.refs_1_, f32[16,16,384]{2,1,0:T(8,128)} %refs_2_.1, f32[2,8,8,384]{3,2,1,0:T(8,128)} %bitcast.4, f32[49,384]{1,0:T(8,128)} %refs_4_.1, f32[384]{0:T(512)} %refs_5_.1, f32[384]{0:T(512)} %refs_6_.1, ...), custom_call_target="tpu_custom_call" | custom-call | tf_op jit(solution)/shard_map/pallas_call | solution.py:626
  15.7 0.8 %shard_map.159 = (f32[2,8,8,384]{3,2,1,0:T(8,128)}, f32[16,16,384]{2,1,0:T(8,128)}) custom-call(f32[3,16,16,128]{3,2,1,0:T(8,128)S(1)} %get-tuple-element.6.obuf, f32[2,8,8,384]{3,2,1,0:T(8,128)S(1)} %get-tuple-element.7.tokout), custom_call_target="tpu_custom_call" | custom-call | tf_op jit(solution)/shard_map/pallas_call | solution.py:650

commit v4 on v3

--- a/solution.py
+++ b/solution.py
@@ -14,27 +14,73 @@
 PAD = 8
 BLOCK = 256
 WIDE = 16
-TABLE, NEAR, GROWS, GFAR, TROWS, TFAR, TNEAR, PASS, PROWS, RAW, RELAY = 0, 1, 2, 4, 5, 7, 8, 9, 10, 12, 13
-SENT_BY = (0, 0, 1, 2, 0, 1, 2, 0, 0, 0, 3, 4, 0, 0)
+TABLE, GROWS, GFAR, TROWS, TFAR, PASS, PROWS, RAW, RELAY = 0, 1, 3, 4, 6, 8, 9, 11, 12
+SENT_BY = (0, 1, 2, 0, 1, 2, 0, 0, 0, 3, 4, 0, 0)
 
 
 def nt_dot(a, b):
     return lax.dot_general(a, b, (((1,), (1,)), ((), ())), preferred_element_type=jnp.float32)
 
 
-def depthwise(src, weight, chunk, taps, side, flip):
+def depthwise_taps(weight, table, chunk, taps, flip):
+    h = [weight[chunk, a * taps : (a + 1) * taps, :] for a in range(taps)]
+    if flip:
+        h = h[::-1]
+    s = [h[0] + h[1], h[2] + h[3], h[4] + h[5], h[6]]
+    rows = [s[0], s[2], s[1], s[3], s[0] + s[1], s[2] + s[3]]
+    rows += [h[0], h[4], h[2], h[6], h[0] + h[2], h[4] + h[6], h[1], h[3], h[5]]
+    for t, row in enumerate(rows):
+        table[chunk, t, :taps] = row
+
+
+def depthwise(src, sums, table, chunk, taps, side, flip):
     half = side // 2
     reach = taps // 2
+    pairs = (side + taps - 1) // 2
+    quads = pairs // 2
+    for i in range(pairs):
+        sums[i] = src[chunk, 2 * i] + src[chunk, 2 * i + 1]
+    for i in range(quads):
+        sums[pairs + i] = sums[2 * i] + sums[2 * i + 1]
+        sums[pairs + quads + i] = src[chunk, 4 * i + 1] + src[chunk, 4 * i + 3]
+
     outs = []
     for parity in range(2):
-        total = None
-        for b in range(taps):
-            rows = src[chunk, :, pl.ds(PAD - reach + parity + b, half, stride=2), :]
-            for a in range(taps):
-                k = (taps - 1 - a) * taps + taps - 1 - b if flip else a * taps + b
-                term = rows[a : a + side] * weight[chunk, k : k + 1, :]
-                total = term if total is None else total + term
-        outs.append(total)
+
+        def leaf(row, tap_ids, count):
+            totals = [None] * count
+            for b in range(taps):
+                cols = pl.ds(PAD - reach + parity + b, half, stride=2)
+                at = taps - 1 - b if flip else b
+                lines = [row(i, cols) for i in range(count + len(tap_ids) - 1)]
+                for j, t in enumerate(tap_ids):
+                    tap = table[chunk, t, at : at + 1, :]
+                    for i in range(count):
+                        term = lines[i + j] * tap
+                        totals[i] = term if totals[i] is None else totals[i] + term
+            return totals
+
+        def nested(odd, even, both, first):
+            n = half // 2
+            f = leaf(odd, (first, first + 1), n)
+            g = leaf(even, (first + 2, first + 3), n + 1)
+            s = leaf(both, (first + 4, first + 5), n)
+            return [f[i // 2] + g[i // 2 + 1] if i % 2 else s[i // 2] - f[i // 2] - g[i // 2] for i in range(half)]
+
+        s = nested(
+            lambda i, cols: sums[2 * i + 1, cols, :],
+            lambda i, cols: sums[2 * i, cols, :],
+            lambda i, cols: sums[pairs + i, cols, :],
+            0,
+        )
+        f = nested(
+            lambda i, cols: src[chunk, 4 * i + 3, cols, :],
+            lambda i, cols: src[chunk, 4 * i + 1, cols, :],
+            lambda i, cols: sums[pairs + quads + i, cols, :],
+            6,
+        )
+        g = leaf(lambda i, cols: src[chunk, 2 * i, cols, :], (12, 13, 14), half + 1)
+        outs.append([f[i // 2] + g[i // 2 + 1] if i % 2 else s[i // 2] - f[i // 2] - g[i // 2] for i in range(side)])
     return outs
 
 
@@ -61,6 +107,9 @@
     def seat(k, which):
         return lax.rem(lax.div(me, 2) + k, pairs) * 2 + which
 
+    def across(k):
+        return seat(k, core if k == 0 else 1 - core)
+
     beyond = {-1: g > 0, 1: g < groups - 1}
 
     for buf in (r.grow, r.gcorn_in, r.arow, r.acorn):
@@ -97,8 +146,14 @@
 
     fetch("owner", (r.owner_hbm, r.owner_ref))
     fetch("tg", (r.tg_hbm, r.tg))
+    by_lane = []
+    for c in range(chunks):
+        lane = slice(c * LANES, (c + 1) * LANES)
+        by_lane.append((r.dww_hbm.at[:, lane], r.dww.at[c]))
+        by_lane.append((r.x_hbm.at[:, :, lane], r.xpad.at[c, reach : reach + side, PAD : PAD + side, :]))
     fetch(
-        "small",
+        "x",
+        *by_lane,
         (r.dwb_hbm, r.dwb),
         (r.gain_hbm, r.gain),
         (r.lnb_hbm, r.lnb),
@@ -107,12 +162,6 @@
         (r.cb_hbm, r.cb),
         (r.bin_hbm, r.bin_),
     )
-    by_lane = []
-    for c in range(chunks):
-        lane = slice(c * LANES, (c + 1) * LANES)
-        by_lane.append((r.dww_hbm.at[:, lane], r.dww.at[c]))
-        by_lane.append((r.x_hbm.at[:, :, lane], r.xpad.at[c, reach : reach + side, PAD : PAD + side, :]))
-    fetch("x", *by_lane)
     fetch("image", (r.image_hbm, r.image_ref))
     fetch("win", (r.win_hbm, r.win))
     fetch("wout", (r.wout_hbm, r.wout))
@@ -155,29 +204,43 @@
     for m in table_moves:
         m.start()
     fetched("tg")
-    near_move = move(r.tg, r.ntg, NEAR, partner)
+    near_move = move(r.tg, r.ntg, TABLE, partner)
     near_move.start()
     upper = half // 2
-    raw_moves = [move(r.tg.at[:, upper:], r.xtg.at[0, k - 1], RAW, seat(k, core)) for k in range(1, pairs)]
+    raw_moves = [move(r.tg.at[:, upper:], r.xtg.at[0, k - 1], RAW, across(k)) for k in range(1, pairs)]
     for m in raw_moves:
         m.start()
 
     def forward_conv(c):
-        outs = depthwise(r.xpad, r.dww, c, taps, side, False)
+        depthwise_taps(r.dww, r.taps, c, taps, False)
+        outs = depthwise(r.xpad, r.sums, r.taps, c, taps, side, False)
         bias = vector(r.dwb, slice(c * LANES, (c + 1) * LANES))
         for parity in range(2):
-            part = (outs[parity] + bias).reshape(half, 2, half, LANES)
-            for row in range(2):
-                r.sp[c, row * 2 + parity] = part[:, row].reshape(cells, LANES)
-
-    fetched("small")
+            for i in range(side):
+                at = i // 2 * half
+                r.sp[c, i % 2 * 2 + parity, at : at + half] = outs[parity][i] + bias
+
     fetched("x")
     for c in range(chunks):
         forward_conv(c)
+    def gelu(n):
+        lane = slice(n * BLOCK, (n + 1) * BLOCK)
+        pre_all = jnp.dot(r.nb[...], r.win[:, lane], preferred_element_type=jnp.float32)
+        bias = vector(r.bin_, lane)
+        pooled = None
+        for q in range(4):
+            pre = pre_all[q * cells : (q + 1) * cells] + bias
+            cdf = 0.5 + 0.5 * lax.erf(pre * math.sqrt(0.5))
+            pdf = jnp.exp(pre * pre * -0.5) * (1.0 / math.sqrt(2.0 * math.pi))
+            r.dg[q * cells : (q + 1) * cells, lane] = cdf + pre * pdf
+            value = pre * cdf
+            pooled = value if pooled is None else pooled + value
+        r.hb[:, lane] = (pooled * 0.25).astype(jnp.bfloat16)
+
     tile = cells * channels
     edge = half * channels
     main = (pairs - 1) * (tile + 2 * edge)
-    masked = (pairs - 1) * upper * 2 * (edge // 2 + channels)
+    masked = (pairs - 1) * (upper * edge + half * channels)
     raw = (pairs - 1) * slots * (half - upper) * edge
     strips = pairs * (edge + 2 * channels)
     for q in range(4):
@@ -195,8 +258,11 @@
                 hat * vector(r.gain, lane) + vector(r.lnb, lane)
             ).astype(jnp.bfloat16)
 
-    settle(r.recv.at[TABLE], (peers - 1) * 8 * LANES)
-    settle(r.recv.at[NEAR], slots * tile)
+    fetched("win")
+    for n in range(hid // BLOCK):
+        gelu(n)
+
+    settle(r.recv.at[TABLE], (peers - 1) * 8 * LANES + slots * tile)
 
     def masks_of(who, device):
         inside = jnp.logical_and(who >= 0, who < peers)
@@ -221,7 +287,7 @@
     def held_far(who):
         pairs_of = []
         for k in range(1, pairs):
-            for via, which in ((0, core), (1, 1 - core)):
+            for via, which in ((0, 1 - core), (1, core)):
                 for s, mask in enumerate(masks_of(who, seat(pairs - k, which))):
                     pairs_of.append((r.xtg.at[via, k - 1, s], wide(mask)))
         return pairs_of
@@ -230,7 +296,7 @@
         return functools.reduce(jnp.add, terms)
 
     for k in range(pairs):
-        home = seat(k, core)
+        home = across(k)
         whole = held(home)
         for part in ((slice(0, half),) if k == 0 else (slice(0, upper), slice(half - 1, half))):
             r.gmain[k, part] = total_of([ref[part] * mask for ref, mask in whole])
@@ -240,17 +306,17 @@
             if k == 0:
                 r.gcols[side_at] = col
             else:
-                r.gfar[k - 1, side_at] = col[:upper]
+                r.gfar[k - 1, side_at] = col[: half // 2]
             for d, at in ((0, 0), (1, half - 1)):
                 r.gcorn[k, d, side_at : side_at + 1, :] = col[at : at + 1]
 
-    def row_moves(src_row, src_corner, dst_row, dst_corner, group, which):
+    def row_moves(src_row, src_corner, dst_row, dst_corner, group, where):
         moves = {}
         for d, dr in ((0, -1), (1, 1)):
             for k in range(pairs):
                 moves[d, k] = (
-                    move(src_row(d, k), dst_row(d, k), group + d, seat(k, which), g + dr),
-                    move(src_corner(d, k), dst_corner(d, k), group + d, seat(k, which), g + dr),
+                    move(src_row(d, k), dst_row(d, k), group + d, where(k), g + dr),
+                    move(src_corner(d, k), dst_corner(d, k), group + d, where(k), g + dr),
                 )
         return moves
 
@@ -276,7 +342,7 @@
         lambda d, k: r.grow.at[d, k],
         lambda d, k: r.gcorn_in.at[d, k],
         GROWS,
-        core,
+        across,
     )
     @pl.when(beyond[1])
     def _():
@@ -285,26 +351,12 @@
     start_rows(g_rows)
     g_far = []
     for k in range(1, pairs):
-        g_far.append(move(r.gfar.at[k - 1], r.rcols.at[k - 1], GFAR, seat(k, core)))
-        g_far.append(move(r.gmain.at[k, :upper], r.rmain.at[k - 1], GFAR, seat(k, core)))
+        g_far.append(move(r.gfar.at[k - 1], r.rcols.at[k - 1], GFAR, across(k)))
+        g_far.append(move(r.gmain.at[k, :upper], r.rmain.at[k - 1], GFAR, across(k)))
 
     for m in g_far:
         m.start()
 
-    fetched("win")
-    for n in range(hid // BLOCK):
-        lane = slice(n * BLOCK, (n + 1) * BLOCK)
-        pre_all = jnp.dot(r.nb[...], r.win[:, lane], preferred_element_type=jnp.float32)
-        bias = vector(r.bin_, lane)
-        pooled = None
-        for q in range(4):
-            pre = pre_all[q * cells : (q + 1) * cells] + bias
-            cdf = 0.5 + 0.5 * lax.erf(pre * math.sqrt(0.5))
-            pdf = jnp.exp(pre * pre * -0.5) * (1.0 / math.sqrt(2.0 * math.pi))
-            r.dg[q * cells : (q + 1) * cells, lane] = cdf + pre * pdf
-            value = pre * cdf
-            pooled = value if pooled is None else pooled + value
-        r.hb[:, lane] = (pooled * 0.25).astype(jnp.bfloat16)
     fetched("wout")
     branch = jnp.dot(r.hb[...], r.wout[...], preferred_element_type=jnp.float32)
     for c in range(chunks):
@@ -333,7 +385,7 @@
         lambda d, k: r.arow.at[d, me],
         lambda d, k: r.acorn.at[d, me],
         TROWS,
-        1 - core,
+        lambda k: seat(k, 1 - core),
     )
     t_far = []
     spans = [slice(at, min(at + 3 * LANES, channels)) for at in range(0, channels, 3 * LANES)]
@@ -349,16 +401,20 @@
             r.ecorn[d, 1:2, lane] = r.beside[at, 0:1, lane]
         sends = []
         for k in range(1, pairs):
-            for ref in (r.acols.at[me, :, :, lane], r.amain.at[me, :, :, lane]):
-                sends.append(move(ref, ref, TFAR, seat(k, 1 - core)))
+            for ref, group in (
+                (r.acols.at[me, :, :, lane], TFAR),
+                (r.amain.at[me, : half // 2, :, lane], TFAR),
+                (r.amain.at[me, half // 2 :, :, lane], TFAR + 1),
+            ):
+                sends.append(move(ref, ref, group, seat(k, 1 - core)))
         if lane is spans[-1]:
             start_rows(t_rows)
         for m in sends:
             m.start()
         t_far += sends
     t_near = [
-        move(r.acols.at[me], r.acols.at[me], TNEAR, partner),
-        move(r.amain.at[me], r.amain.at[me], TNEAR, partner),
+        move(r.acols.at[me], r.acols.at[me], PASS, partner),
+        move(r.amain.at[me], r.amain.at[me], PASS, partner),
     ]
     for m in t_near:
         m.start()
@@ -367,6 +423,12 @@
     relay = move(r.xtg.at[0], r.xtg.at[1], RELAY, partner)
     relay.start()
 
+    for c in range(chunks):
+        depthwise_taps(r.dww, r.taps, c, taps, True)
+
+    for n in range(hid // BLOCK):
+        lane = slice(n * BLOCK, (n + 1) * BLOCK)
+        r.woutt[:, lane] = r.wout[lane].T
     for a in range(3):
         for b in range(3):
             at, flipped = (a * 3 + b) * channels, ((2 - a) * 3 + 2 - b) * channels
@@ -393,7 +455,7 @@
     r.grid_g[1 : 1 + upper, inner, :] = total_of([r.gmain[0, :upper]] + [r.rmain[k] for k in range(pairs - 1)])
     for side_at, at in ((0, PAD - 1), (1, PAD + half)):
         r.grid_g[1 : 1 + upper, at, :] = total_of(
-            [r.gcols[side_at, :upper]] + [r.rcols[k, side_at] for k in range(pairs - 1)]
+            [r.gcols[side_at, :upper]] + [r.rcols[k, side_at, :upper] for k in range(pairs - 1)]
         )
     for d, row in ((1, 0), (0, half + 1)):
         r.grid_g[row, inner, :] = total_of([r.grow[d, k] for k in range(pairs)]) * keep[d]
@@ -415,7 +477,7 @@
 
     for n in range(hid // BLOCK):
         lane = slice(n * BLOCK, (n + 1) * BLOCK)
-        dh = nt_dot(scaled, r.wout[lane, :])
+        dh = jnp.dot(scaled, r.woutt[:, lane], preferred_element_type=jnp.float32)
         for q in range(4):
             rows = slice(q * cells, (q + 1) * cells)
             r.dpb[rows, lane] = (dh * r.dg[rows, lane]).astype(jnp.bfloat16)
@@ -433,44 +495,42 @@
                 r.gpad[c, reach + 2 * i + q // 2, pl.ds(PAD + q % 2, half, stride=2), :] = back[i]
 
     def backward_conv(c):
-        outs = depthwise(r.gpad, r.dww, c, taps, side, True)
-        direct = jnp.broadcast_to(r.gq[c][:, None], (half, 2, half, LANES)).reshape(side, half, LANES)
+        outs = depthwise(r.gpad, r.sums, r.taps, c, taps, side, True)
         for parity in range(2):
-            value = outs[parity] + direct
             for i in range(side):
-                r.obuf[c, i, pl.ds(parity, half, stride=2), :] = value[i]
-
+                r.obuf[c, i, pl.ds(parity, half, stride=2), :] = outs[parity][i] + r.gq[c, i // 2]
+
+    def pass_on(part):
+        if part == 0:
+            received_rows(TROWS)
+            for d, dr in ((0, -1), (1, 1)):
+
+                @pl.when(beyond[-dr])
+                def _():
+                    for k in range(pairs):
+                        who = seat(k, 1 - core)
+                        for ref in (r.arow.at[d, who], r.acorn.at[d, who]):
+                            move(ref, ref, PROWS + d, partner).start()
+
+        settle(r.recv.at[TFAR + part], main - (pairs - 1) * (tile // 2) if part == 0 else (pairs - 1) * (tile // 2))
+        for k in range(1, pairs):
+            who = seat(k, 1 - core)
+            if part == 0:
+                refs = (r.acols.at[who], r.amain.at[who, : half // 2])
+            else:
+                refs = (r.amain.at[who, half // 2 :],)
+            for ref in refs:
+                move(ref, ref, PASS, partner).start()
+
+    pass_on(0)
     backward_conv(0)
-
-    received_rows(TROWS)
-    settle(r.recv.at[TFAR], main)
-    passed = []
-    for k in range(1, pairs):
-        who = seat(k, 1 - core)
-        passed.append(move(r.acols.at[who], r.acols.at[who], PASS, partner))
-        passed.append(move(r.amain.at[who], r.amain.at[who], PASS, partner))
-    for m in passed:
-        m.start()
-    passed_rows = {}
-    for d, dr in ((0, -1), (1, 1)):
-        for k in range(pairs):
-            who = seat(k, 1 - core)
-            passed_rows[d, k] = (
-                move(r.arow.at[d, who], r.arow.at[d, who], PROWS + d, partner),
-                move(r.acorn.at[d, who], r.acorn.at[d, who], PROWS + d, partner),
-            )
-
-        @pl.when(beyond[-dr])
-        def _():
-            for k in range(pairs):
-                for m in passed_rows[d, k]:
-                    m.start()
-
-    for c in range(1, chunks):
-        backward_conv(c)
-
-    settle(r.recv.at[TNEAR], tile + 2 * edge)
-    settle(r.recv.at[PASS], main)
+    pass_on(1)
+    backward_conv(1)
+    backward_conv(2)
+    chosen = [[wide(mask) for mask in masks_of(p, me)] for p in range(peers)]
+    bias = vector(r.cb)
+
+    settle(r.recv.at[PASS], main + tile + 2 * edge)
     received_rows(PROWS)
 
     settle(r.send.at[0], (peers - 1) * 8 * LANES + slots * tile + 2 * raw + masked + 2 * main + tile + 2 * edge)
@@ -484,8 +544,6 @@
         def _():
             settle(r.send.at[3 + d], strips)
 
-    chosen = [[wide(mask) for mask in masks_of(p, me)] for p in range(peers)]
-    bias = vector(r.cb)
     for s in range(slots):
         total = None
         west = jnp.zeros((half, channels), jnp.float32)
@@ -543,6 +601,7 @@
         cells = half * half
         chunks = channels // LANES
         assert width == side and llm_peer.shape == (1, 1)
+        assert taps == 7 and side % 4 == 0
         f32, bf16 = jnp.float32, jnp.bfloat16
         padded = (chunks, side + 2 * (taps // 2), side + 2 * PAD, LANES)
         block = (half, half, channels)
@@ -568,11 +627,13 @@
             "tokout": buf(slots, *block),
         }
         sent = (slots + 1) * cells * channels + 2 * half * channels + peers * 8 * LANES
-        sent += (pairs - 1) * (3 * (cells + 2 * half) + 2 * slots * cells) * channels
-        span = max(sent, (side * side + taps * taps) * channels) // LANES
+        sent += (pairs - 1) * (3 * (cells + 2 * half) + 3 * slots * cells) * channels
+        span = max(sent, (side * side + taps * taps + 6) * channels + hid) // LANES
         scratch = {
             "xpad": buf(*padded),
             "gpad": buf(*padded),
+            "sums": buf((side + taps - 1) // 2 + (side + taps - 1) // 4 * 2, side + 2 * PAD, LANES),
+            "taps": buf(chunks, 2 * taps + 1, 8, LANES),
             "dww": buf(chunks, taps * taps, LANES),
             "gq": buf(chunks, half, half, LANES),
             "dwb": buf(channels),
@@ -583,6 +644,7 @@
             "cb": buf(channels),
             "bin_": buf(hid),
             "win": buf(*w_in.shape, kind=bf16),
+            "woutt": buf(channels, hid, kind=bf16),
             "wout": buf(*w_out.shape, kind=bf16),
             "cw": buf(9 * channels, channels, kind=bf16),
             "cwt": buf(9 * channels, channels, kind=bf16),
@@ -616,11 +678,11 @@
             "acorn": buf(2, peers, *tip),
             "image_ref": pltpu.SMEM(image_of_row.shape, jnp.int32),
             "owner_ref": pltpu.SMEM((1, 1), jnp.int32),
-            "in_sems": dma(8),
+            "in_sems": dma(7),
             "hello": pltpu.SemaphoreType.REGULAR,
             "send": dma(5),
             "span": buf(span, 1, LANES),
-            "recv": dma(14),
+            "recv": dma(13),
         }
         names = inputs + tuple(held) + tuple(scratch)
         state = pl.pallas_call(

time: 16.7 us -> 16.4 us (0.982)
  Pallas kernels: 15.2 us -> 15 us
    pallas_call x1, Pallas kernels: 14.4 us -> 14.1 us  [on_device(): pl.pallas_call(functools.partial(kernel, groups, peers, taps, names), out...]
where the time goes in v4:
time: 16.4 us; the launch traced here: 16.3 us
  Pallas kernels  15 us (91%)
  between operations  1.29 us (8%)
    pallas_call x1, Pallas kernels, on_device(): pl.pallas_call(functools.partial(kernel, groups, peers, taps, names), out...  14.1 us
    pallas_call x1, Pallas kernels, on_device(): pl.pallas_call(tail, out_shape=(jax.ShapeDtypeStruct((slots,) + block, f3...  0.84 us

profile of v4, /device:TPU:0, one launch (start us, length us, event | category | flops | bytes accessed | tf_op | source)
XLA Modules:
  0.0 16.3 jit_solution(15481518664839471737)
XLA Ops:
  1.3 14.1 %shard_map.158 = (f32[3,16,16,128]{3,2,1,0:T(8,128)S(1)}, f32[2,8,8,384]{3,2,1,0:T(8,128)S(1)}) custom-call(s32[8]{0:T(128)} %refs_0_.1, s32[1,1]{1,0:T(1,128)S(6)} %copy.17.refs_1_, f32[16,16,384]{2,1,0:T(8,128)} %refs_2_.1, f32[2,8,8,384]{3,2,1,0:T(8,128)} %bitcast.4, f32[49,384]{1,0:T(8,128)} %refs_4_.1, f32[384]{0:T(512)} %refs_5_.1, f32[384]{0:T(512)} %refs_6_.1, ...), custom_call_target="tpu_custom_call" | custom-call | tf_op jit(solution)/shard_map/pallas_call | solution.py:688
  15.4 0.8 %shard_map.159 = (f32[2,8,8,384]{3,2,1,0:T(8,128)}, f32[16,16,384]{2,1,0:T(8,128)}) custom-call(f32[3,16,16,128]{3,2,1,0:T(8,128)S(1)} %get-tuple-element.6.obuf, f32[2,8,8,384]{3,2,1,0:T(8,128)S(1)} %get-tuple-element.7.tokout), custom_call_target="tpu_custom_call" | custom-call | tf_op jit(solution)/shard_map/pallas_call | solution.py:712
